TPU v7x, 512 devices: a whole 4x8x8 slice. The times are simulated.
512 devices in a mesh: section: 4 (over y_hi), dp: 32 (over x, z), space: 4 (over y_lo, core).
Axes of the slice: x: 4, y: 8 (y_hi: 4, y_lo: 2; y = y_hi * 2 + y_lo), z: 8, core: 2. Of those that a mesh axis runs over, the one named last changes fastest.
Arguments:
- enc_input: bfloat16 [4, 32, 32, 8, 8, 128], P('section', 'dp', None, 'space'), may hold values from -6 to 6
- dec_input: bfloat16 [4, 32, 32, 8, 8, 128], P('section', 'dp', None, None, 'space'), may hold values from -6 to 6
- dec_cotangent: bfloat16 [4, 32, 32, 8, 8, 128], P('section', 'dp', None, None, 'space'), may hold values from -6 to 6
- deep_cotangent: bfloat16 [4, 32, 32, 8, 8, 128], P('section', 'dp', None, 'space'), may hold values from -6 to 6
- enc_weight: bfloat16 [4, 27, 32, 32], P('section'), may hold values from -0.21875 to 0.21875
- dec_weight: bfloat16 [4, 27, 32, 64], P('section'), may hold values from -0.15625 to 0.15625
- enc_gain: float32 [4, 32], P('section'), may hold values from 0.25 to 1.75
- enc_bias: float32 [4, 32], P('section'), may hold values from -2 to 2
- dec_gain: float32 [4, 32], P('section'), may hold values from 0.25 to 1.75
- dec_bias: float32 [4, 32], P('section'), may hold values from -2 to 2
Outputs:
- enc_handoff: bfloat16 [4, 32, 32, 8, 8, 128], P('section', 'dp', None, 'space')
- dec_handoff: bfloat16 [4, 32, 32, 8, 8, 128], P('section', 'dp', None, None, 'space')
- enc_weight_grad: float32 [4, 27648], P('section', ('dp', 'space'))
- dec_weight_grad: float32 [4, 55296], P('section', ('dp', 'space'))
All inputs are finite; a program needn't handle non-finite values.
Results may differ from a plain program's by a relative error of at most 0.0075.
Values may be sent and summed in bfloat16 or wider, within the bound.
A program may use at most 64 MiB of HBM per device.

v0:
```python
import math

import jax
import jax.numpy as jnp
from jax import lax
from jax.sharding import Mesh
from jax.sharding import PartitionSpec as P

SPACE = ("space_0", "space_1")
DP = ("dp_0", "dp_1")
DP_SPACE = ("dp_0", "dp_1", "space_0", "space_1")


EPS = 1e-05


def padded_2(cells, sides, width):
    for axis, dim in sides:
        count = lax.axis_size(axis)
        ends = count - 1
        head = lax.slice_in_dim(cells, 0, width, axis=dim)
        tail = lax.slice_in_dim(cells, cells.shape[dim] - width, cells.shape[dim], axis=dim)
        cells = jnp.concatenate(
            [
                lax.ppermute(tail, axis, [(i, (i + 1) % count) for i in range(ends)]),
                cells,
                lax.ppermute(head, axis, [((i + 1) % count, i) for i in range(ends)]),
            ],
            axis=dim,
        )
    return cells


def copy_for_each(array, axis):
    count = lax.axis_size(axis)
    return lax.all_to_all(
        jnp.broadcast_to(array[None], (count, *array.shape)), axis, 0, 0, tiled=True
    )


def of_everyone(array, axis):
    return copy_for_each(array, axis).sum(axis=0)


def in_one(arrays, axis):
    ends = [0]
    for a in arrays:
        ends.append(ends[-1] + a.size)
    subtotal = of_everyone(jnp.concatenate([a.ravel() for a in arrays]), axis)
    return tuple((subtotal[b:e].reshape(a.shape) for a, b, e in zip(arrays, ends, ends[1:])))


def shifted_2(block, axis, distance):
    devices = range(lax.axis_size(axis))
    route = [(i - distance, i) for i in devices if i - distance in devices]
    return lax.ppermute(block, axis, route)


def split_up(array, dim, count):
    before, after = (array.shape[:dim], array.shape[dim + 1 :])
    return jnp.moveaxis(array.reshape(*before, count, -1, *after), dim, 0)


def summed_on_arrival(array, axis, dim):
    blocks = split_up(array, dim, lax.axis_size(axis))
    arrived = lax.all_to_all(blocks, axis, split_axis=0, concat_axis=0, tiled=True)
    return arrived.sum(axis=0)


def sum_by_axis(array, axes, dim):
    far, near = axes
    blocks = split_up(array, dim, lax.axis_size(far))
    nearer = summed_on_arrival(blocks, near, dim + 1)
    arrived = lax.all_to_all(nearer, far, split_axis=0, concat_axis=0, tiled=True)
    return arrived.sum(axis=0)


def convolve(padded, weights):
    depth_cells = padded.shape[1] - 2
    height_cells = padded.shape[2] - 2
    width_cells = padded.shape[3] - 2
    summed = jnp.zeros((weights.shape[1], depth_cells, height_cells, width_cells), jnp.float32)
    for depth_tap in range(3):
        for height_tap in range(3):
            shifted = jnp.stack(
                [
                    padded[
                        :,
                        depth_tap : depth_tap + depth_cells,
                        height_tap : height_tap + height_cells,
                        width_tap : width_tap + width_cells,
                    ]
                    for width_tap in range(3)
                ]
            )
            first = depth_tap * 9 + height_tap * 3
            tap_weights = weights[first : first + 3]
            summed = summed + jnp.einsum(
                "koi,kidhw->odhw", tap_weights, shifted, preferred_element_type=jnp.float32
            )
    return summed


def weight_terms(padded, cotangent):
    depth_cells = cotangent.shape[1]
    height_cells = cotangent.shape[2]
    width_cells = cotangent.shape[3]
    pieces = []
    for depth_tap in range(3):
        for height_tap in range(3):
            shifted = jnp.stack(
                [
                    padded[
                        :,
                        depth_tap : depth_tap + depth_cells,
                        height_tap : height_tap + height_cells,
                        width_tap : width_tap + width_cells,
                    ]
                    for width_tap in range(3)
                ]
            )
            pieces.append(
                jnp.einsum(
                    "odhw,kidhw->koi", cotangent, shifted, preferred_element_type=jnp.float32
                )
            )
    return jnp.concatenate(pieces, axis=0)


def channel_view(values):
    return values[:, None, None, None]


def body(
    enc_input,
    dec_input,
    dec_cotangent,
    deep_cotangent,
    enc_weight,
    dec_weight,
    enc_gain,
    enc_bias,
    dec_gain,
    dec_bias,
):
    volume = enc_input[0, 0]
    channels = volume.shape[0]
    slabs = lax.axis_size(SPACE)
    voxels = volume.shape[1] * slabs * volume.shape[2] * volume.shape[3]
    grad_scale = 1.0 / math.sqrt(lax.axis_size(DP) * voxels)
    enc_rimmed = padded_2(volume, ((SPACE, 1),), 1)
    enc_padded = jnp.pad(enc_rimmed, ((0, 0), (0, 0), (1, 1), (1, 1)))
    enc_pre = convolve(enc_padded, enc_weight[0])
    enc_sums, enc_squares = in_one(
        (jnp.sum(enc_pre, axis=(1, 2, 3)), jnp.sum(enc_pre * enc_pre, axis=(1, 2, 3))), SPACE
    )
    enc_mean = enc_sums / voxels
    enc_scale = lax.rsqrt(enc_squares / voxels - enc_mean * enc_mean + EPS)
    enc_hat = (enc_pre - channel_view(enc_mean)) * channel_view(enc_scale)
    enc_normed = channel_view(enc_gain[0]) * enc_hat + channel_view(enc_bias[0])
    skip_act = jnp.maximum(enc_normed, 0.0).astype(jnp.bfloat16)
    enc_handoff = shifted_2(skip_act[None, None], "section", 1)
    skip_high = lax.all_to_all(skip_act, SPACE, split_axis=2, concat_axis=1, tiled=True)
    joined = jnp.concatenate([dec_input[0, 0], skip_high], axis=0)
    dec_rimmed = padded_2(joined, ((SPACE, 2),), 1)
    dec_padded = jnp.pad(dec_rimmed, ((0, 0), (1, 1), (0, 0), (1, 1)))
    dec_pre = convolve(dec_padded, dec_weight[0])
    dec_sums, dec_squares = in_one(
        (jnp.sum(dec_pre, axis=(1, 2, 3)), jnp.sum(dec_pre * dec_pre, axis=(1, 2, 3))), SPACE
    )
    dec_mean = dec_sums / voxels
    dec_scale = lax.rsqrt(dec_squares / voxels - dec_mean * dec_mean + EPS)
    dec_hat = (dec_pre - channel_view(dec_mean)) * channel_view(dec_scale)
    dec_act = jnp.maximum(
        channel_view(dec_gain[0]) * dec_hat + channel_view(dec_bias[0]), 0.0
    ).astype(jnp.bfloat16)
    dec_handoff = shifted_2(dec_act[None, None], "section", -1)
    cotangent = dec_cotangent[0, 0]
    dec_grad = weight_terms(dec_padded, cotangent).reshape(-1) * grad_scale
    flipped = jnp.swapaxes(dec_weight[0][::-1, :, channels:], 1, 2)
    cot_rimmed = padded_2(cotangent, ((SPACE, 2),), 1)
    cot_padded = jnp.pad(cot_rimmed, ((0, 0), (1, 1), (0, 0), (1, 1)))
    grad_high = convolve(cot_padded, flipped).astype(jnp.bfloat16)
    skip_grad = lax.all_to_all(grad_high, SPACE, split_axis=1, concat_axis=2, tiled=True)
    upstream = skip_grad.astype(jnp.float32) + deep_cotangent[0, 0].astype(jnp.float32)
    gated = jnp.where(enc_normed > 0, upstream, 0.0) * channel_view(enc_gain[0])
    first_sum, second_sum = in_one(
        (jnp.sum(gated, axis=(1, 2, 3)), jnp.sum(gated * enc_hat, axis=(1, 2, 3))), SPACE
    )
    enc_pre_grad = (
        (gated - channel_view(first_sum / voxels) - enc_hat * channel_view(second_sum / voxels))
        * channel_view(enc_scale)
    ).astype(jnp.bfloat16)
    enc_grad = weight_terms(enc_padded, enc_pre_grad).reshape(-1) * grad_scale
    enc_part, dec_part = (
        sum_by_axis(enc_grad, (("dp_0", "dp_1", "space_0"), "space_1"), 0),
        sum_by_axis(dec_grad, (("dp_0", "dp_1", "space_0"), "space_1"), 0),
    )
    return (enc_handoff, dec_handoff, enc_part[None], dec_part[None])


def solution(mesh):
    split = Mesh(
        mesh.devices.reshape(mesh.shape["section"], 4, 8, 2, 2),
        ("section", "dp_0", "dp_1", "space_0", "space_1"),
    )
    placed = (
        P("section", DP, None, SPACE, None, None),
        P("section", DP, None, None, SPACE, None),
        P("section", DP, None, None, SPACE, None),
        P("section", DP, None, SPACE, None, None),
        P("section", None, None, None),
        P("section", None, None, None),
        P("section", None),
        P("section", None),
        P("section", None),
        P("section", None),
    )
    return jax.shard_map(
        body,
        mesh=split,
        in_specs=placed,
        out_specs=(
            P("section", DP, None, SPACE, None, None),
            P("section", DP, None, None, SPACE, None),
            P("section", DP_SPACE),
            P("section", DP_SPACE),
        ),
        check_vma=False,
    )
```

profile of v0, /device:TPU:16, one launch (start us, length us, event | category | flops | bytes accessed | tf_op | source)
XLA Modules:
  0.0 137.5 jit_solution(6968468909326626398)
XLA Ops:
  1.6 1.7 %collective-permute-start.6 = (bf16[32,8,1,128]{3,0,2,1:T(8,128)(2,1)S(1)}, bf16[32,8,1,128]{3,0,2,1:T(8,128)(2,1)S(1)}, u32[]{:S(2)}, u32[]{:S(2)}) collective-permute-start(bf16[32,8,1,128]{3,0,2,1:T(8,128)(2,1)S(1)} %get-tuple-element.113), channel_id=1, source_target_pairs={{0,1},{1,2},{2,3},{4,5},{5,6},{6,7},{8,9},{9,10},{10,11},{12,13},{... | collective-permute-start | bytes 196616 | tf_op jit(solution)/shard_map/ppermute | solution.py:25
  3.3 1.3 collective-permute-start.7
  5.6 4.4 %collective-permute-start = (bf16[32,1,8,128]{3,0,2,1:T(8,128)(2,1)S(1)}, bf16[32,1,8,128]{3,0,2,1:T(8,128)(2,1)S(1)}, u32[]{:S(2)}, u32[]{:S(2)}) collective-permute-start(bf16[32,1,8,128]{3,0,2,1:T(8,128)(2,1)S(1)} %get-tuple-element.119), channel_id=1, source_target_pairs={{0,1},{1,2},{2,3},{4,5},{5,6},{6,7},{8,9},{9,10},{10,11},{12,13},{... | collective-permute-start | bytes 196616 | tf_op jit(solution)/shard_map/ppermute | solution.py:25
  10.0 1.3 collective-permute-start.1
  22.3 5.2 %all-to-all-start = ((f32[4,1,64]{2,1,0:T(1,128)}), f32[4,1,64]{2,1,0:T(1,128)S(1)}, u32[]{:S(2)}, u32[]{:S(2)}) async-start(f32[4,1,64]{2,1,0:T(1,128)} %broadcast_in_dim.16), calls=%async_computation | async-start | bytes 4096 | tf_op jit(solution)/shard_map/all_to_all | solution.py:36
  27.5 2.1 %fusion.39 = bf16[32,8,2,128]{3,0,2,1:T(8,128)(2,1)} fusion(bf16[1,32,8,2,128]{4,1,0,3,2:T(8,128)(2,1)} %get-tuple-element.75, bf16[1,32,8,2,128]{4,1,0,3,2:T(8,128)(2,1)} %get-tuple-element.76, bf16[1,32,8,2,128]{4,1,0,3,2:T(8,128)(2,1)} %get-tuple-element.77, f32[8,2,128,32]{2,3,0,1:T(8,128)S(1)} %convolution_bitcast_fusion, ...), kind=kOutput, calls=%fused_computation.80 | convolution fusion | flops 14352384 | bytes 2646016 | tf_op jit(solution)/shard_map/koi,kidhw->odhw/dot_general | solution.py:98
  29.6 1.6 %all-to-all-done = f32[4,1,64]{2,1,0:T(1,128)S(1)} async-done(((f32[4,1,64]{2,1,0:T(1,128)}), f32[4,1,64]{2,1,0:T(1,128)S(1)}, u32[]{:S(2)}, u32[]{:S(2)}) %all-to-all-start) | async-done | bytes 1056 | tf_op jit(solution)/shard_map/all_to_all | solution.py:36
  31.2 3.3 %all-to-all-start.3 = ((bf16[32,8,2,128]{3,0,2,1:T(8,128)(2,1)}), bf16[32,8,2,128]{3,0,2,1:T(8,128)(2,1)S(1)}, u32[]{:S(2)}, u32[]{:S(2)}) async-start(bf16[32,8,2,128]{3,0,2,1:T(8,128)(2,1)} %fusion.39), calls=%async_computation.3 | async-start | bytes 262144 | tf_op jit(solution)/shard_map/all_to_all | solution.py:184
  34.7 4.5 %all-to-all-done.3 = bf16[32,8,2,128]{3,0,2,1:T(8,128)(2,1)S(1)} async-done(((bf16[32,8,2,128]{3,0,2,1:T(8,128)(2,1)}), bf16[32,8,2,128]{3,0,2,1:T(8,128)(2,1)S(1)}, u32[]{:S(2)}, u32[]{:S(2)}) %all-to-all-start.3) | async-done | bytes 131104 | tf_op jit(solution)/shard_map/all_to_all | solution.py:184
  41.1 3.2 %all-to-all-start.4 = ((f32[4,1,64]{2,1,0:T(1,128)}), f32[4,1,64]{2,1,0:T(1,128)S(1)}, u32[]{:S(2)}, u32[]{:S(2)}) async-start(f32[4,1,64]{2,1,0:T(1,128)} %broadcast_in_dim.20), calls=%async_computation.4 | async-start | bytes 4096 | tf_op jit(solution)/shard_map/all_to_all | solution.py:36
  45.1 2.9 %all-to-all-done.4 = f32[4,1,64]{2,1,0:T(1,128)S(1)} async-done(((f32[4,1,64]{2,1,0:T(1,128)}), f32[4,1,64]{2,1,0:T(1,128)S(1)}, u32[]{:S(2)}, u32[]{:S(2)}) %all-to-all-start.4) | async-done | bytes 1056 | tf_op jit(solution)/shard_map/all_to_all | solution.py:36
  48.0 3.3 %all-to-all-start.1 = ((bf16[32,2,8,128]{3,0,1,2:T(8,128)(2,1)}), bf16[32,2,8,128]{3,0,1,2:T(8,128)(2,1)S(1)}, u32[]{:S(2)}, u32[]{:S(2)}) async-start(bf16[32,2,8,128]{3,0,1,2:T(8,128)(2,1)} %copy.245), calls=%async_computation.1 | async-start | bytes 262144 | tf_op jit(solution)/shard_map/all_to_all | solution.py:163
  56.0 1.9 %collective-permute-start.3 = (bf16[64,8,1,128]{3,0,2,1:T(8,128)(2,1)S(1)}, bf16[64,8,1,128]{3,0,2,1:T(8,128)(2,1)S(1)}, u32[]{:S(2)}, u32[]{:S(2)}) collective-permute-start(bf16[64,8,1,128]{3,0,2,1:T(8,128)(2,1)S(1)} %get-tuple-element.107), channel_id=1, source_target_pairs={{0,1},{1,2},{2,3},{4,5},{5,6},{6,7},{8,9},{9,10},{10,11},{12,13},{... | collective-permute-start | bytes 393224 | tf_op jit(solution)/shard_map/ppermute | solution.py:25
  60.6 3.6 %all-to-all-start.5 = ((f32[2,64,216]{2,1,0:T(8,128)}), f32[2,64,216]{2,1,0:T(8,128)S(1)}, u32[]{:S(2)}, u32[]{:S(2)}) async-start(f32[2,64,216]{2,1,0:T(8,128)} %copy.299), calls=%async_computation.5 | async-start | bytes 262144 | tf_op jit(solution)/shard_map/all_to_all | solution.py:66
  65.1 1.3 slice_bitcast_fusion.20
  76.7 1.7 %fusion.179 = (f32[32]{0:T(128)S(1)}, f32[32]{0:T(128)S(1)}, f32[8,2,128,32]{2,3,1,0:T(8,128)S(1)}) fusion(f32[8,2,128,32]{2,3,0,1:T(8,128)} %convolution_bitcast_fusion.9, f32[8,2,128,32]{2,3,0,1:T(8,128)} %convolution_bitcast_fusion.10, f32[8,2,128,32]{2,3,0,1:T(8,128)} %convolution_bitcast_fusion.11, f32[8,2,128,32]{2,3,0,1:T(8,128)} %convolution_bitcast_fusion.12, ...), kind=kOutput, calls=%fused_computation.389 | convolution fusion | flops 28245952 | bytes 3170560 | tf_op jit(solution)/shard_map/koi,kidhw->odhw/dot_general | solution.py:98
  78.5 5.7 %all_to_all.73 = f32[2,64,432]{2,1,0:T(8,128)S(1)} all-to-all(f32[2,64,432]{2,1,0:T(8,128)S(1)} %bitcast.779), channel_id=1, replica_groups=mesh['section'=4,'dp_0'=4,'dp_1'=8,'space_0'=2,'space_1'=2] {'space_1'}, dimensions={0} | all-to-all | bytes 442368 | tf_op jit(solution)/shard_map/all_to_all | solution.py:66
  84.7 3.4 %all-to-all-start.2 = ((f32[4,1,64]{2,1,0:T(1,128)}), f32[4,1,64]{2,1,0:T(1,128)S(1)}, u32[]{:S(2)}, u32[]{:S(2)}) async-start(f32[4,1,64]{2,1,0:T(1,128)} %broadcast_in_dim.18), calls=%async_computation.2 | async-start | bytes 4096 | tf_op jit(solution)/shard_map/all_to_all | solution.py:36
  88.1 4.8 %collective-permute-start.2 = (bf16[1,1,32,2,8,128]{5,2,4,3,1,0:T(8,128)(2,1)S(1)}, bf16[1,1,32,2,8,128]{5,2,4,3,1,0:T(8,128)(2,1)S(1)}, u32[]{:S(2)}, u32[]{:S(2)}) collective-permute-start(bf16[1,1,32,2,8,128]{5,2,4,3,1,0:T(8,128)(2,1)S(1)} %bitcast.781), channel_id=1, source_target_pairs={{0,128},{128,256},{256,384},{1,129},{129,257},{257,385},{2,130},{1... | collective-permute-start | bytes 393224 | tf_op jit(solution)/shard_map/ppermute | solution.py:56
  94.4 15.2 %all-to-all-start.6 = ((f32[64,1,216]{2,1,0:T(1,128)}), f32[64,1,216]{2,1,0:T(1,128)S(1)}, u32[]{:S(2)}, u32[]{:S(2)}) async-start(f32[64,1,216]{2,1,0:T(1,128)} %all_to_all.59), calls=%async_computation.6 | async-start | bytes 131072 | tf_op jit(solution)/shard_map/all_to_all | solution.py:74
  109.8 10.3 %all-to-all-done.6 = f32[64,1,216]{2,1,0:T(1,128)S(1)} async-done(((f32[64,1,216]{2,1,0:T(1,128)}), f32[64,1,216]{2,1,0:T(1,128)S(1)}, u32[]{:S(2)}, u32[]{:S(2)}) %all-to-all-start.6) | async-done | bytes 55328 | tf_op jit(solution)/shard_map/all_to_all | solution.py:74
  120.1 4.6 %all-to-all-start.8 = ((f32[64,1,432]{2,1,0:T(1,128)}), f32[64,1,432]{2,1,0:T(1,128)S(1)}, u32[]{:S(2)}, u32[]{:S(2)}) async-start(f32[64,1,432]{2,1,0:T(1,128)} %all_to_all.62), calls=%async_computation.8 | async-start | bytes 262144 | tf_op jit(solution)/shard_map/all_to_all | solution.py:74
  124.9 1.9 %collective-permute-start.5 = (bf16[1,1,32,8,2,128]{5,2,4,3,1,0:T(8,128)(2,1)S(1)}, bf16[1,1,32,8,2,128]{5,2,4,3,1,0:T(8,128)(2,1)S(1)}, u32[]{:S(2)}, u32[]{:S(2)}) collective-permute-start(bf16[1,1,32,8,2,128]{5,2,4,3,1,0:T(8,128)(2,1)S(1)} %fusion.103), channel_id=1, source_target_pairs={{128,0},{256,128},{384,256},{129,1},{257,129},{385,257},{130,2},{2... | collective-permute-start | bytes 393224 | tf_op jit(solution)/shard_map/ppermute | solution.py:56
  128.2 7.8 %collective-permute-done.5 = bf16[1,1,32,8,2,128]{5,2,4,3,1,0:T(8,128)(2,1)S(1)} collective-permute-done((bf16[1,1,32,8,2,128]{5,2,4,3,1,0:T(8,128)(2,1)S(1)}, bf16[1,1,32,8,2,128]{5,2,4,3,1,0:T(8,128)(2,1)S(1)}, u32[]{:S(2)}, u32[]{:S(2)}) %collective-permute-start.5) | collective-permute-done | bytes 131104 | tf_op jit(solution)/shard_map/ppermute | solution.py:56
  (212 shorter events, 38.5 us)
Async XLA Ops:
  1.6 10.9 %collective-permute-start.6 = (bf16[32,8,1,128]{3,0,2,1:T(8,128)(2,1)S(1)}, bf16[32,8,1,128]{3,0,2,1:T(8,128)(2,1)S(1)}, u32[]{:S(2)}, u32[]{:S(2)}) collective-permute-start(bf16[32,8,1,128]{3,0,2,1:T(8,128)(2,1)S(1)} %get-tuple-element.113), channel_id=1, source_target_pairs={{0,1},{1,2},{2,3},{4,5},{5,6},{6,7},{8,9},{9,10},{10,11},{12,13},{... | collective-permute-start | bytes 196616 | tf_op jit(solution)/shard_map/ppermute | solution.py:25
  3.3 9.2 %collective-permute-start.7 = (bf16[32,8,1,128]{3,0,2,1:T(8,128)(2,1)S(1)}, bf16[32,8,1,128]{3,0,2,1:T(8,128)(2,1)S(1)}, u32[]{:S(2)}, u32[]{:S(2)}) collective-permute-start(bf16[32,8,1,128]{3,0,2,1:T(8,128)(2,1)S(1)} %get-tuple-element.114), channel_id=1, source_target_pairs={{1,0},{2,1},{3,2},{5,4},{6,5},{7,6},{9,8},{10,9},{11,10},{13,12},{... | collective-permute-start | bytes 196616 | tf_op jit(solution)/shard_map/ppermute | solution.py:27
  5.6 8.7 %collective-permute-start = (bf16[32,1,8,128]{3,0,2,1:T(8,128)(2,1)S(1)}, bf16[32,1,8,128]{3,0,2,1:T(8,128)(2,1)S(1)}, u32[]{:S(2)}, u32[]{:S(2)}) collective-permute-start(bf16[32,1,8,128]{3,0,2,1:T(8,128)(2,1)S(1)} %get-tuple-element.119), channel_id=1, source_target_pairs={{0,1},{1,2},{2,3},{4,5},{5,6},{6,7},{8,9},{9,10},{10,11},{12,13},{... | collective-permute-start | bytes 196616 | tf_op jit(solution)/shard_map/ppermute | solution.py:25
  10.0 4.4 %collective-permute-start.1 = (bf16[32,1,8,128]{3,0,2,1:T(8,128)(2,1)S(1)}, bf16[32,1,8,128]{3,0,2,1:T(8,128)(2,1)S(1)}, u32[]{:S(2)}, u32[]{:S(2)}) collective-permute-start(bf16[32,1,8,128]{3,0,2,1:T(8,128)(2,1)S(1)} %get-tuple-element.120), channel_id=1, source_target_pairs={{1,0},{2,1},{3,2},{5,4},{6,5},{7,6},{9,8},{10,9},{11,10},{13,12},{... | collective-permute-start | bytes 196616 | tf_op jit(solution)/shard_map/ppermute | solution.py:27
  22.3 8.9 %all-to-all-start = ((f32[4,1,64]{2,1,0:T(1,128)}), f32[4,1,64]{2,1,0:T(1,128)S(1)}, u32[]{:S(2)}, u32[]{:S(2)}) async-start(f32[4,1,64]{2,1,0:T(1,128)} %broadcast_in_dim.16), calls=%async_computation | async-start | bytes 4096 | tf_op jit(solution)/shard_map/all_to_all | solution.py:36
  27.5 11.7 %copy-start.44 = (f32[1,32]{1,0:T(1,128)S(1)}, f32[1,32]{1,0:T(1,128)}, u32[]{:S(2)}) copy-start(f32[1,32]{1,0:T(1,128)} %param.17) | copy-start | bytes 388
  27.5 11.7 %copy-start.45 = (f32[1,32]{1,0:T(1,128)S(1)}, f32[1,32]{1,0:T(1,128)}, u32[]{:S(2)}) copy-start(f32[1,32]{1,0:T(1,128)} %param.16) | copy-start | bytes 388
  29.6 14.8 %copy-start.42 = (bf16[1,1,32,8,2,128]{5,4,3,2,1,0:T(2,128)(2,1)S(1)}, bf16[1,1,32,8,2,128]{5,4,3,2,1,0:T(2,128)(2,1)}, u32[]{:S(2)}) copy-start(bf16[1,1,32,8,2,128]{5,4,3,2,1,0:T(2,128)(2,1)} %param.11) | copy-start | bytes 393220
  31.2 7.9 %all-to-all-start.3 = ((bf16[32,8,2,128]{3,0,2,1:T(8,128)(2,1)}), bf16[32,8,2,128]{3,0,2,1:T(8,128)(2,1)S(1)}, u32[]{:S(2)}, u32[]{:S(2)}) async-start(bf16[32,8,2,128]{3,0,2,1:T(8,128)(2,1)} %fusion.39), calls=%async_computation.3 | async-start | bytes 262144 | tf_op jit(solution)/shard_map/all_to_all | solution.py:184
  39.1 12.5 %copy-start.31 = (bf16[1,32,2,8,128]{4,1,0,3,2:T(8,128)(2,1)S(1)}, bf16[1,32,2,8,128]{4,1,0,3,2:T(8,128)(2,1)}, u32[]{:S(2)}) copy-start(bf16[1,32,2,8,128]{4,1,0,3,2:T(8,128)(2,1)} %copy-done.30) | copy-start | bytes 393220
  39.2 12.5 %copy-start.33 = (bf16[1,32,2,8,128]{4,1,0,3,2:T(8,128)(2,1)S(1)}, bf16[1,32,2,8,128]{4,1,0,3,2:T(8,128)(2,1)}, u32[]{:S(2)}) copy-start(bf16[1,32,2,8,128]{4,1,0,3,2:T(8,128)(2,1)} %copy-done.32) | copy-start | bytes 393220
  39.2 12.5 %copy-start.35 = (bf16[1,32,2,8,128]{4,1,0,3,2:T(8,128)(2,1)S(1)}, bf16[1,32,2,8,128]{4,1,0,3,2:T(8,128)(2,1)}, u32[]{:S(2)}) copy-start(bf16[1,32,2,8,128]{4,1,0,3,2:T(8,128)(2,1)} %copy-done.34) | copy-start | bytes 393220
  41.1 6.9 %all-to-all-start.4 = ((f32[4,1,64]{2,1,0:T(1,128)}), f32[4,1,64]{2,1,0:T(1,128)S(1)}, u32[]{:S(2)}, u32[]{:S(2)}) async-start(f32[4,1,64]{2,1,0:T(1,128)} %broadcast_in_dim.20), calls=%async_computation.4 | async-start | bytes 4096 | tf_op jit(solution)/shard_map/all_to_all | solution.py:36
  48.0 7.9 %all-to-all-start.1 = ((bf16[32,2,8,128]{3,0,1,2:T(8,128)(2,1)}), bf16[32,2,8,128]{3,0,1,2:T(8,128)(2,1)S(1)}, u32[]{:S(2)}, u32[]{:S(2)}) async-start(bf16[32,2,8,128]{3,0,1,2:T(8,128)(2,1)} %copy.245), calls=%async_computation.1 | async-start | bytes 262144 | tf_op jit(solution)/shard_map/all_to_all | solution.py:163
  56.0 8.2 %collective-permute-start.3 = (bf16[64,8,1,128]{3,0,2,1:T(8,128)(2,1)S(1)}, bf16[64,8,1,128]{3,0,2,1:T(8,128)(2,1)S(1)}, u32[]{:S(2)}, u32[]{:S(2)}) collective-permute-start(bf16[64,8,1,128]{3,0,2,1:T(8,128)(2,1)S(1)} %get-tuple-element.107), channel_id=1, source_target_pairs={{0,1},{1,2},{2,3},{4,5},{5,6},{6,7},{8,9},{9,10},{10,11},{12,13},{... | collective-permute-start | bytes 393224 | tf_op jit(solution)/shard_map/ppermute | solution.py:25
  57.9 6.2 %collective-permute-start.4 = (bf16[64,8,1,128]{3,0,2,1:T(8,128)(2,1)S(1)}, bf16[64,8,1,128]{3,0,2,1:T(8,128)(2,1)S(1)}, u32[]{:S(2)}, u32[]{:S(2)}) collective-permute-start(bf16[64,8,1,128]{3,0,2,1:T(8,128)(2,1)S(1)} %get-tuple-element.108), channel_id=1, source_target_pairs={{1,0},{2,1},{3,2},{5,4},{6,5},{7,6},{9,8},{10,9},{11,10},{13,12},{... | collective-permute-start | bytes 393224 | tf_op jit(solution)/shard_map/ppermute | solution.py:27
  60.6 17.9 %all-to-all-start.5 = ((f32[2,64,216]{2,1,0:T(8,128)}), f32[2,64,216]{2,1,0:T(8,128)S(1)}, u32[]{:S(2)}, u32[]{:S(2)}) async-start(f32[2,64,216]{2,1,0:T(8,128)} %copy.299), calls=%async_computation.5 | async-start | bytes 262144 | tf_op jit(solution)/shard_map/all_to_all | solution.py:66
  78.4 46.3 %copy-start.46 = (f32[1,32]{1,0:T(1,128)S(1)}, f32[1,32]{1,0:T(1,128)}, u32[]{:S(2)}) copy-start(f32[1,32]{1,0:T(1,128)} %param.19) | copy-start | bytes 388
  78.4 46.3 %copy-start.47 = (f32[1,32]{1,0:T(1,128)S(1)}, f32[1,32]{1,0:T(1,128)}, u32[]{:S(2)}) copy-start(f32[1,32]{1,0:T(1,128)} %param.18) | copy-start | bytes 388
  84.7 9.7 %all-to-all-start.2 = ((f32[4,1,64]{2,1,0:T(1,128)}), f32[4,1,64]{2,1,0:T(1,128)S(1)}, u32[]{:S(2)}, u32[]{:S(2)}) async-start(f32[4,1,64]{2,1,0:T(1,128)} %broadcast_in_dim.18), calls=%async_computation.2 | async-start | bytes 4096 | tf_op jit(solution)/shard_map/all_to_all | solution.py:36
  88.1 39.3 %collective-permute-start.2 = (bf16[1,1,32,2,8,128]{5,2,4,3,1,0:T(8,128)(2,1)S(1)}, bf16[1,1,32,2,8,128]{5,2,4,3,1,0:T(8,128)(2,1)S(1)}, u32[]{:S(2)}, u32[]{:S(2)}) collective-permute-start(bf16[1,1,32,2,8,128]{5,2,4,3,1,0:T(8,128)(2,1)S(1)} %bitcast.781), channel_id=1, source_target_pairs={{0,128},{128,256},{256,384},{1,129},{129,257},{257,385},{2,130},{1... | collective-permute-start | bytes 393224 | tf_op jit(solution)/shard_map/ppermute | solution.py:56
  94.4 25.7 %all-to-all-start.6 = ((f32[64,1,216]{2,1,0:T(1,128)}), f32[64,1,216]{2,1,0:T(1,128)S(1)}, u32[]{:S(2)}, u32[]{:S(2)}) async-start(f32[64,1,216]{2,1,0:T(1,128)} %all_to_all.59), calls=%async_computation.6 | async-start | bytes 131072 | tf_op jit(solution)/shard_map/all_to_all | solution.py:74
  120.1 16.7 %all-to-all-start.8 = ((f32[64,1,432]{2,1,0:T(1,128)}), f32[64,1,432]{2,1,0:T(1,128)S(1)}, u32[]{:S(2)}, u32[]{:S(2)}) async-start(f32[64,1,432]{2,1,0:T(1,128)} %all_to_all.62), calls=%async_computation.8 | async-start | bytes 262144 | tf_op jit(solution)/shard_map/all_to_all | solution.py:74
  124.9 11.2 %collective-permute-start.5 = (bf16[1,1,32,8,2,128]{5,2,4,3,1,0:T(8,128)(2,1)S(1)}, bf16[1,1,32,8,2,128]{5,2,4,3,1,0:T(8,128)(2,1)S(1)}, u32[]{:S(2)}, u32[]{:S(2)}) collective-permute-start(bf16[1,1,32,8,2,128]{5,2,4,3,1,0:T(8,128)(2,1)S(1)} %fusion.103), channel_id=1, source_target_pairs={{128,0},{256,128},{384,256},{129,1},{257,129},{385,257},{130,2},{2... | collective-permute-start | bytes 393224 | tf_op jit(solution)/shard_map/ppermute | solution.py:56
  (40 other events, 124.3 us)
where the time goes:
time: 139 us; the launch traced here: 137 us
  starting transfers between devices  60.6 us (44%)
  waiting for transfers between devices  27.7 us (20%)
  matrix products  19.3 us (14%)
  local copies, waits for them, and re-layouts  16.9 us (12%)
  blocking collectives  5.68 us (4%)
  other arithmetic  5.57 us (4%)
  between operations  1.77 us (1%)
    all_to_all x2, starting transfers between devices, sum_by_axis(): lax.all_to_all(nearer, far, split_axis=0, concat_axis=0, tiled=True)  19.8 us
    dot_general x27, matrix products, convolve(): jnp.einsum('koi,kidhw->odhw', tap_weights, shifted, preferred_element_typ...  13.4 us
    all_to_all x3, starting transfers between devices, copy_for_each(): lax.all_to_all(jnp.broadcast_to(array[None], (count, *array.shape)), axis...  11.8 us
    all_to_all x2, waiting for transfers between devices, sum_by_axis(): lax.all_to_all(nearer, far, split_axis=0, concat_axis=0, tiled=True)  10.3 us
    ppermute x3, starting transfers between devices, padded_2(): lax.ppermute(tail, axis, [(i, (i + 1) % count) for i in range(ends)])  8.07 us
    ppermute x2, waiting for transfers between devices, shifted_2(): return lax.ppermute(block, axis, route)  7.84 us
    unnamed x102, local copies, waits for them, and re-layouts  7.25 us
    ppermute x2, starting transfers between devices, shifted_2(): return lax.ppermute(block, axis, route)  6.73 us
  transfers between devices with their start and end apart: 16, of which 6 were waited for; matrix products, arithmetic and copies ran while one was open for 19% of the time, Pallas kernels for 0%

commit v1 on v0

--- a/solution.py
+++ b/solution.py
@@ -3,12 +3,13 @@
 import jax
 import jax.numpy as jnp
 from jax import lax
-from jax.sharding import Mesh
+from jax.experimental import pallas as pl
+from jax.experimental.pallas import tpu as pltpu
 from jax.sharding import PartitionSpec as P
 
-SPACE = ("space_0", "space_1")
-DP = ("dp_0", "dp_1")
-DP_SPACE = ("dp_0", "dp_1", "space_0", "space_1")
+SPACE = "space"
+DP = "dp"
+DP_SPACE = ("dp", "space")
 
 
 EPS = 1e-05
@@ -56,23 +57,111 @@
     return lax.ppermute(block, axis, route)
 
 
-def split_up(array, dim, count):
-    before, after = (array.shape[:dim], array.shape[dim + 1 :])
-    return jnp.moveaxis(array.reshape(*before, count, -1, *after), dim, 0)
-
-
-def summed_on_arrival(array, axis, dim):
-    blocks = split_up(array, dim, lax.axis_size(axis))
-    arrived = lax.all_to_all(blocks, axis, split_axis=0, concat_axis=0, tiled=True)
-    return arrived.sum(axis=0)
-
-
-def sum_by_axis(array, axes, dim):
-    far, near = axes
-    blocks = split_up(array, dim, lax.axis_size(far))
-    nearer = summed_on_arrival(blocks, near, dim + 1)
-    arrived = lax.all_to_all(nearer, far, split_axis=0, concat_axis=0, tiled=True)
-    return arrived.sum(axis=0)
+def reduce_kernel(n_dp, n_space, terms, total, arrived, near, partial, sent, got, near_sent, near_got):
+    me = lax.axis_index(DP)
+    slab = lax.axis_index(SPACE)
+    barrier = pltpu.get_barrier_semaphore()
+
+    def greet(i, carry):
+        pl.semaphore_signal(barrier, inc=1, device_id={DP: lax.rem(me + i, n_dp)})
+        return carry
+
+    lax.fori_loop(1, n_dp, greet, 0)
+    for i in range(1, n_space):
+        pl.semaphore_signal(barrier, inc=1, device_id={SPACE: lax.rem(slab + i, n_space)})
+    pl.semaphore_wait(barrier, n_dp + n_space - 2)
+
+    def far_copy(i):
+        peer = lax.rem(me + i, n_dp)
+        return pltpu.make_async_remote_copy(
+            src_ref=terms.at[peer],
+            dst_ref=arrived.at[me],
+            send_sem=sent.at[peer],
+            recv_sem=got.at[me],
+            device_id={DP: peer},
+        )
+
+    def far_arrival(i):
+        peer = lax.rem(me - i + n_dp, n_dp)
+        return peer, pltpu.make_async_remote_copy(
+            src_ref=terms.at[peer],
+            dst_ref=arrived.at[peer],
+            send_sem=sent.at[peer],
+            recv_sem=got.at[peer],
+            device_id={DP: peer},
+        )
+
+    def start(i, carry):
+        far_copy(i).start()
+        return carry
+
+    lax.fori_loop(1, n_dp, start, 0)
+
+    def collect(i, acc):
+        peer, copy = far_arrival(i)
+        copy.wait_recv()
+        return acc + arrived[peer]
+
+    partial[...] = lax.fori_loop(1, n_dp, collect, terms[me])
+
+    def near_copy(i):
+        peer = lax.rem(slab + i, n_space)
+        return pltpu.make_async_remote_copy(
+            src_ref=partial,
+            dst_ref=near.at[i - 1],
+            send_sem=near_sent.at[i - 1],
+            recv_sem=near_got.at[i - 1],
+            device_id={SPACE: peer},
+        )
+
+    for i in range(1, n_space):
+        near_copy(i).start()
+    acc = partial[...]
+    for i in range(1, n_space):
+        near_copy(i).wait_recv()
+        acc = acc + near[i - 1]
+    total[...] = acc
+
+    def drain(i, carry):
+        far_copy(i).wait_send()
+        return carry
+
+    lax.fori_loop(1, n_dp, drain, 0)
+    for i in range(1, n_space):
+        near_copy(i).wait_send()
+
+
+def reduced(enc_grad, dec_grad):
+    n_dp, n_space = lax.axis_size(DP), lax.axis_size(SPACE)
+    enc_terms = enc_grad.reshape(n_dp, -1)
+    dec_terms = dec_grad.reshape(n_dp, -1)
+    enc_width, dec_width = enc_terms.shape[1], dec_terms.shape[1]
+    rows = -(-(enc_width + dec_width) // 1024) * 8
+    terms = jnp.concatenate([enc_terms, dec_terms], axis=1)
+    terms = jnp.pad(terms, ((0, 0), (0, rows * 128 - terms.shape[1]))).reshape(n_dp, rows, 128)
+    vmem = pl.BlockSpec(memory_space=pltpu.VMEM)
+    total = pl.pallas_call(
+        lambda *refs: reduce_kernel(n_dp, n_space, *refs),
+        out_shape=jax.ShapeDtypeStruct((rows, 128), jnp.float32),
+        in_specs=[vmem],
+        out_specs=vmem,
+        scratch_shapes=[
+            pltpu.VMEM((n_dp, rows, 128), jnp.float32),
+            pltpu.VMEM((n_space - 1, rows, 128), jnp.float32),
+            pltpu.VMEM((rows, 128), jnp.float32),
+            pltpu.SemaphoreType.DMA((n_dp,)),
+            pltpu.SemaphoreType.DMA((n_dp,)),
+            pltpu.SemaphoreType.DMA((n_space - 1,)),
+            pltpu.SemaphoreType.DMA((n_space - 1,)),
+        ],
+        compiler_params=pltpu.CompilerParams(collective_id=0, has_side_effects=True),
+    )(terms).reshape(-1)
+    slab = lax.axis_index(SPACE)
+    enc_part = lax.dynamic_slice(total, (slab * (enc_width // n_space),), (enc_width // n_space,))
+    dec_part = lax.dynamic_slice(
+        total, (enc_width + slab * (dec_width // n_space),), (dec_width // n_space,)
+    )
+    return enc_part, dec_part
 
 
 def convolve(padded, weights):
@@ -192,18 +281,11 @@
         * channel_view(enc_scale)
     ).astype(jnp.bfloat16)
     enc_grad = weight_terms(enc_padded, enc_pre_grad).reshape(-1) * grad_scale
-    enc_part, dec_part = (
-        sum_by_axis(enc_grad, (("dp_0", "dp_1", "space_0"), "space_1"), 0),
-        sum_by_axis(dec_grad, (("dp_0", "dp_1", "space_0"), "space_1"), 0),
-    )
+    enc_part, dec_part = reduced(enc_grad, dec_grad)
     return (enc_handoff, dec_handoff, enc_part[None], dec_part[None])
 
 
 def solution(mesh):
-    split = Mesh(
-        mesh.devices.reshape(mesh.shape["section"], 4, 8, 2, 2),
-        ("section", "dp_0", "dp_1", "space_0", "space_1"),
-    )
     placed = (
         P("section", DP, None, SPACE, None, None),
         P("section", DP, None, None, SPACE, None),
@@ -218,7 +300,7 @@
     )
     return jax.shard_map(
         body,
-        mesh=split,
+        mesh=mesh,
         in_specs=placed,
         out_specs=(
             P("section", DP, None, SPACE, None, None),

time: 139 us -> 121 us (0.87)
  the two profiles are of different devices: /device:TPU:16 before, /device:TPU:1 now
where the time goes in v1:
time: 121 us; the launch traced here: 120 us
  starting transfers between devices  42.2 us (35%)
  Pallas kernels  29.1 us (24%)
  local copies, waits for them, and re-layouts  18.9 us (16%)
  matrix products  15.2 us (13%)
  waiting for transfers between devices  8.46 us (7%)
  other arithmetic  4.3 us (4%)
  between operations  1.73 us (1%)
    pallas_call x1, Pallas kernels, reduced(): pl.pallas_call(lambda *refs: reduce_kernel(n_dp, n_space, *refs), out_sha...  29.1 us
    all_to_all x3, starting transfers between devices, copy_for_each(): lax.all_to_all(jnp.broadcast_to(array[None], (count, *array.shape)), axis...  10.7 us
    ppermute x3, starting transfers between devices, padded_2(): lax.ppermute(tail, axis, [(i, (i + 1) % count) for i in range(ends)])  10 us
    ppermute x3, starting transfers between devices, padded_2(): lax.ppermute(head, axis, [((i + 1) % count, i) for i in range(ends)])  9.96 us
    unnamed x111, local copies, waits for them, and re-layouts  9.29 us
    dot_general x27, matrix products, convolve(): jnp.einsum('koi,kidhw->odhw', tap_weights, shifted, preferred_element_typ...  9.27 us
    dot_general x18, matrix products, weight_terms(): jnp.einsum('odhw,kidhw->koi', cotangent, shifted, preferred_element_type=...  5.97 us
    all_to_all x1, starting transfers between devices, body(): lax.all_to_all(grad_high, SPACE, split_axis=1, concat_axis=2, tiled=True)  3.98 us
  transfers between devices with their start and end apart: 13, of which 5 were waited for; matrix products, arithmetic and copies ran while one was open for 12% of the time, Pallas kernels for 24%

profile of v1, /device:TPU:1, one launch (start us, length us, event | category | flops | bytes accessed | tf_op | source)
XLA Modules:
  0.0 119.9 jit_solution(5387825414775692368)
XLA Ops:
  0.6 0.9 copy.475
  1.6 4.6 %collective-permute-start.6 = (bf16[32,8,1,128]{3,0,2,1:T(8,128)(2,1)S(1)}, bf16[32,8,1,128]{3,0,2,1:T(8,128)(2,1)S(1)}, u32[]{:S(2)}, u32[]{:S(2)}) collective-permute-start(bf16[32,8,1,128]{3,0,2,1:T(8,128)(2,1)S(1)} %get-tuple-element.113), channel_id=1, source_target_pairs={{0,1},{1,2},{2,3},{4,5},{5,6},{6,7},{8,9},{9,10},{10,11},{12,13},{... | collective-permute-start | bytes 196616 | tf_op jit(solution)/shard_map/ppermute | solution.py:26
  6.2 5.5 %collective-permute-start.7 = (bf16[32,8,1,128]{3,0,2,1:T(8,128)(2,1)S(1)}, bf16[32,8,1,128]{3,0,2,1:T(8,128)(2,1)S(1)}, u32[]{:S(2)}, u32[]{:S(2)}) collective-permute-start(bf16[32,8,1,128]{3,0,2,1:T(8,128)(2,1)S(1)} %get-tuple-element.114), channel_id=1, source_target_pairs={{1,0},{2,1},{3,2},{5,4},{6,5},{7,6},{9,8},{10,9},{11,10},{13,12},{... | collective-permute-start | bytes 196616 | tf_op jit(solution)/shard_map/ppermute | solution.py:28
  12.6 1.9 %collective-permute-start = (bf16[32,1,8,128]{3,0,2,1:T(8,128)(2,1)S(1)}, bf16[32,1,8,128]{3,0,2,1:T(8,128)(2,1)S(1)}, u32[]{:S(2)}, u32[]{:S(2)}) collective-permute-start(bf16[32,1,8,128]{3,0,2,1:T(8,128)(2,1)S(1)} %get-tuple-element.119), channel_id=1, source_target_pairs={{0,1},{1,2},{2,3},{4,5},{5,6},{6,7},{8,9},{9,10},{10,11},{12,13},{... | collective-permute-start | bytes 196616 | tf_op jit(solution)/shard_map/ppermute | solution.py:26
  14.5 2.4 %collective-permute-start.1 = (bf16[32,1,8,128]{3,0,2,1:T(8,128)(2,1)S(1)}, bf16[32,1,8,128]{3,0,2,1:T(8,128)(2,1)S(1)}, u32[]{:S(2)}, u32[]{:S(2)}) collective-permute-start(bf16[32,1,8,128]{3,0,2,1:T(8,128)(2,1)S(1)} %get-tuple-element.120), channel_id=1, source_target_pairs={{1,0},{2,1},{3,2},{5,4},{6,5},{7,6},{9,8},{10,9},{11,10},{13,12},{... | collective-permute-start | bytes 196616 | tf_op jit(solution)/shard_map/ppermute | solution.py:28
  17.0 1.2 copy.265
  28.9 3.2 %all-to-all-start = ((f32[4,1,64]{2,1,0:T(1,128)}), f32[4,1,64]{2,1,0:T(1,128)S(1)}, u32[]{:S(2)}, u32[]{:S(2)}) async-start(f32[4,1,64]{2,1,0:T(1,128)} %broadcast_in_dim.16), calls=%async_computation | async-start | bytes 4096 | tf_op jit(solution)/shard_map/all_to_all | solution.py:37
  32.2 2.1 %fusion.39 = bf16[32,8,2,128]{3,0,2,1:T(8,128)(2,1)} fusion(bf16[1,32,8,2,128]{4,1,0,3,2:T(8,128)(2,1)} %get-tuple-element.75, bf16[1,32,8,2,128]{4,1,0,3,2:T(8,128)(2,1)} %get-tuple-element.76, bf16[1,32,8,2,128]{4,1,0,3,2:T(8,128)(2,1)} %get-tuple-element.77, f32[8,2,128,32]{2,3,0,1:T(8,128)S(1)} %convolution_bitcast_fusion, ...), kind=kOutput, calls=%fused_computation.80 | convolution fusion | flops 14352384 | bytes 2646016 | tf_op jit(solution)/shard_map/koi,kidhw->odhw/dot_general | solution.py:187
  34.9 4.0 %all-to-all-start.3 = ((bf16[32,8,2,128]{3,0,2,1:T(8,128)(2,1)}), bf16[32,8,2,128]{3,0,2,1:T(8,128)(2,1)S(1)}, u32[]{:S(2)}, u32[]{:S(2)}) async-start(bf16[32,8,2,128]{3,0,2,1:T(8,128)(2,1)} %fusion.39), calls=%async_computation.3 | async-start | bytes 262144 | tf_op jit(solution)/shard_map/all_to_all | solution.py:273
  38.9 3.5 %all-to-all-done.3 = bf16[32,8,2,128]{3,0,2,1:T(8,128)(2,1)S(1)} async-done(((bf16[32,8,2,128]{3,0,2,1:T(8,128)(2,1)}), bf16[32,8,2,128]{3,0,2,1:T(8,128)(2,1)S(1)}, u32[]{:S(2)}, u32[]{:S(2)}) %all-to-all-start.3) | async-done | bytes 131104 | tf_op jit(solution)/shard_map/all_to_all | solution.py:273
  42.5 1.3 %fusion.179 = (f32[32]{0:T(128)S(1)}, f32[32]{0:T(128)S(1)}, f32[32,2,8,128]{3,0,2,1:T(8,128)S(1)}, bf16[32,2,8,128]{3,0,2,1:T(8,128)(2,1)S(1)}) fusion(f32[32]{0:T(128)S(1)} %get-tuple-element.126, f32[2,8,128,32]{2,3,1,0:T(8,128)S(1)} %get-tuple-element.127, f32[32]{0:T(128)S(1)} %get-tuple-element.125, f32[32,2,8,128]{3,0,2,1:T(8,128)S(1)} %bitcast.779, ...), kind=kLoop, calls=%fused_computation.390 | loop fusion | flops 917440 | bytes 1049344 | tf_op jit(solution)/shard_map/reduce_sum | solution.py:277
  44.4 4.2 %all-to-all-start.4 = ((f32[4,1,64]{2,1,0:T(1,128)}), f32[4,1,64]{2,1,0:T(1,128)S(1)}, u32[]{:S(2)}, u32[]{:S(2)}) async-start(f32[4,1,64]{2,1,0:T(1,128)} %broadcast_in_dim.20), calls=%async_computation.4 | async-start | bytes 4096 | tf_op jit(solution)/shard_map/all_to_all | solution.py:37
  49.4 2.4 %collective-permute-start.2 = (bf16[1,1,32,2,8,128]{5,2,4,3,1,0:T(8,128)(2,1)S(1)}, bf16[1,1,32,2,8,128]{5,2,4,3,1,0:T(8,128)(2,1)S(1)}, u32[]{:S(2)}, u32[]{:S(2)}) collective-permute-start(bf16[1,1,32,2,8,128]{5,2,4,3,1,0:T(8,128)(2,1)S(1)} %bitcast.781), channel_id=1, source_target_pairs={{0,128},{128,256},{256,384},{1,129},{129,257},{257,385},{2,130},{1... | collective-permute-start | bytes 393224 | tf_op jit(solution)/shard_map/ppermute | solution.py:57
  51.8 3.9 %all-to-all-start.1 = ((bf16[32,2,8,128]{3,0,1,2:T(8,128)(2,1)}), bf16[32,2,8,128]{3,0,1,2:T(8,128)(2,1)S(1)}, u32[]{:S(2)}, u32[]{:S(2)}) async-start(bf16[32,2,8,128]{3,0,1,2:T(8,128)(2,1)} %copy.241), calls=%async_computation.1 | async-start | bytes 262144 | tf_op jit(solution)/shard_map/all_to_all | solution.py:252
  60.1 3.5 %collective-permute-start.3 = (bf16[64,8,1,128]{3,0,2,1:T(8,128)(2,1)S(1)}, bf16[64,8,1,128]{3,0,2,1:T(8,128)(2,1)S(1)}, u32[]{:S(2)}, u32[]{:S(2)}) collective-permute-start(bf16[64,8,1,128]{3,0,2,1:T(8,128)(2,1)S(1)} %get-tuple-element.107), channel_id=1, source_target_pairs={{0,1},{1,2},{2,3},{4,5},{5,6},{6,7},{8,9},{9,10},{10,11},{12,13},{... | collective-permute-start | bytes 393224 | tf_op jit(solution)/shard_map/ppermute | solution.py:26
  63.7 2.1 %collective-permute-start.4 = (bf16[64,8,1,128]{3,0,2,1:T(8,128)(2,1)S(1)}, bf16[64,8,1,128]{3,0,2,1:T(8,128)(2,1)S(1)}, u32[]{:S(2)}, u32[]{:S(2)}) collective-permute-start(bf16[64,8,1,128]{3,0,2,1:T(8,128)(2,1)S(1)} %get-tuple-element.108), channel_id=1, source_target_pairs={{1,0},{2,1},{3,2},{5,4},{6,5},{7,6},{9,8},{10,9},{11,10},{13,12},{... | collective-permute-start | bytes 393224 | tf_op jit(solution)/shard_map/ppermute | solution.py:28
  66.9 3.1 %collective-permute-done.4 = bf16[64,8,1,128]{3,0,2,1:T(8,128)(2,1)S(1)} collective-permute-done((bf16[64,8,1,128]{3,0,2,1:T(8,128)(2,1)S(1)}, bf16[64,8,1,128]{3,0,2,1:T(8,128)(2,1)S(1)}, u32[]{:S(2)}, u32[]{:S(2)}) %collective-permute-start.4) | collective-permute-done | bytes 131104 | tf_op jit(solution)/shard_map/ppermute | solution.py:28
  71.0 1.3 %slice_bitcast_fusion.20 = (bf16[1,64,8,2,128]{4,1,3,2,0:T(8,128)(2,1)S(1)}, bf16[1,64,8,2,128]{4,1,3,2,0:T(8,128)(2,1)S(1)}, bf16[1,64,8,2,128]{4,1,3,2,0:T(8,1...) fusion(bf16[64,10,4,130]{3,0,2,1:T(8,128)(2,1)S(1)} %select_max, ...), kind=kLoop, calls=%fused_computation.217 | loop fusion | bytes 9961472 | tf_op jit(solution)/shard_map/stack | solution.py:174
  79.9 3.2 %all-to-all-start.2 = ((f32[4,1,64]{2,1,0:T(1,128)}), f32[4,1,64]{2,1,0:T(1,128)S(1)}, u32[]{:S(2)}, u32[]{:S(2)}) async-start(f32[4,1,64]{2,1,0:T(1,128)} %broadcast_in_dim.18), calls=%async_computation.2 | async-start | bytes 4096 | tf_op jit(solution)/shard_map/all_to_all | solution.py:37
  83.5 1.1 all-to-all-done.2
  84.9 1.3 %collective-permute-start.5 = (bf16[1,1,32,8,2,128]{5,2,4,3,1,0:T(8,128)(2,1)S(1)}, bf16[1,1,32,8,2,128]{5,2,4,3,1,0:T(8,128)(2,1)S(1)}, u32[]{:S(2)}, u32[]{:S(2)}) collective-permute-start(bf16[1,1,32,8,2,128]{5,2,4,3,1,0:T(8,128)(2,1)S(1)} %fusion.104), channel_id=1, source_target_pairs={{128,0},{256,128},{384,256},{129,1},{257,129},{385,257},{130,2},{2... | collective-permute-start | bytes 393224 | tf_op jit(solution)/shard_map/ppermute | solution.py:57
  87.4 29.1 %shard_map.129 = f32[24,128]{1,0:T(8,128)} custom-call(f32[32,24,128]{2,1,0:T(8,128)} %bitcast.778), custom_call_target="tpu_custom_call" | custom-call | tf_op jit(solution)/shard_map/pallas_call | solution.py:143
  116.5 1.4 %dynamic_slice.7 = f32[432]{0:T(512)} dynamic-slice(f32[3072]{0:T(1024)} %bitcast.784, s32[]{:T(128)S(6)} %select_n.12), dynamic_slice_sizes={432} | dynamic-slice | bytes 3460 | tf_op jit(solution)/shard_map/dynamic_slice | solution.py:161
  117.8 1.3 %dynamic_slice.6 = f32[216]{0:T(256)} dynamic-slice(f32[3072]{0:T(1024)} %bitcast.785, s32[]{:T(128)S(6)} %select_n.11), dynamic_slice_sizes={216} | dynamic-slice | bytes 1732 | tf_op jit(solution)/shard_map/dynamic_slice | solution.py:160
  (210 shorter events, 29.8 us)
Async XLA Ops:
  1.6 16.6 %collective-permute-start.6 = (bf16[32,8,1,128]{3,0,2,1:T(8,128)(2,1)S(1)}, bf16[32,8,1,128]{3,0,2,1:T(8,128)(2,1)S(1)}, u32[]{:S(2)}, u32[]{:S(2)}) collective-permute-start(bf16[32,8,1,128]{3,0,2,1:T(8,128)(2,1)S(1)} %get-tuple-element.113), channel_id=1, source_target_pairs={{0,1},{1,2},{2,3},{4,5},{5,6},{6,7},{8,9},{9,10},{10,11},{12,13},{... | collective-permute-start | bytes 196616 | tf_op jit(solution)/shard_map/ppermute | solution.py:26
  6.2 12.0 %collective-permute-start.7 = (bf16[32,8,1,128]{3,0,2,1:T(8,128)(2,1)S(1)}, bf16[32,8,1,128]{3,0,2,1:T(8,128)(2,1)S(1)}, u32[]{:S(2)}, u32[]{:S(2)}) collective-permute-start(bf16[32,8,1,128]{3,0,2,1:T(8,128)(2,1)S(1)} %get-tuple-element.114), channel_id=1, source_target_pairs={{1,0},{2,1},{3,2},{5,4},{6,5},{7,6},{9,8},{10,9},{11,10},{13,12},{... | collective-permute-start | bytes 196616 | tf_op jit(solution)/shard_map/ppermute | solution.py:28
  12.6 7.4 %collective-permute-start = (bf16[32,1,8,128]{3,0,2,1:T(8,128)(2,1)S(1)}, bf16[32,1,8,128]{3,0,2,1:T(8,128)(2,1)S(1)}, u32[]{:S(2)}, u32[]{:S(2)}) collective-permute-start(bf16[32,1,8,128]{3,0,2,1:T(8,128)(2,1)S(1)} %get-tuple-element.119), channel_id=1, source_target_pairs={{0,1},{1,2},{2,3},{4,5},{5,6},{6,7},{8,9},{9,10},{10,11},{12,13},{... | collective-permute-start | bytes 196616 | tf_op jit(solution)/shard_map/ppermute | solution.py:26
  14.5 5.6 %collective-permute-start.1 = (bf16[32,1,8,128]{3,0,2,1:T(8,128)(2,1)S(1)}, bf16[32,1,8,128]{3,0,2,1:T(8,128)(2,1)S(1)}, u32[]{:S(2)}, u32[]{:S(2)}) collective-permute-start(bf16[32,1,8,128]{3,0,2,1:T(8,128)(2,1)S(1)} %get-tuple-element.120), channel_id=1, source_target_pairs={{1,0},{2,1},{3,2},{5,4},{6,5},{7,6},{9,8},{10,9},{11,10},{13,12},{... | collective-permute-start | bytes 196616 | tf_op jit(solution)/shard_map/ppermute | solution.py:28
  22.2 5.6 %copy-start.26 = (bf16[1,32,2,8,128]{4,1,0,3,2:T(8,128)(2,1)}, bf16[1,32,2,8,128]{4,1,0,3,2:T(8,128)(2,1)S(1)}, u32[]{:S(2)}) copy-start(bf16[1,32,2,8,128]{4,1,0,3,2:T(8,128)(2,1)S(1)} %get-tuple-element.79) | copy-start | bytes 393220
  28.9 5.9 %all-to-all-start = ((f32[4,1,64]{2,1,0:T(1,128)}), f32[4,1,64]{2,1,0:T(1,128)S(1)}, u32[]{:S(2)}, u32[]{:S(2)}) async-start(f32[4,1,64]{2,1,0:T(1,128)} %broadcast_in_dim.16), calls=%async_computation | async-start | bytes 4096 | tf_op jit(solution)/shard_map/all_to_all | solution.py:37
  32.1 10.3 %copy-start.48 = (f32[1,32]{1,0:T(1,128)S(1)}, f32[1,32]{1,0:T(1,128)}, u32[]{:S(2)}) copy-start(f32[1,32]{1,0:T(1,128)} %param.17) | copy-start | bytes 388
  32.2 10.3 %copy-start.49 = (f32[1,32]{1,0:T(1,128)S(1)}, f32[1,32]{1,0:T(1,128)}, u32[]{:S(2)}) copy-start(f32[1,32]{1,0:T(1,128)} %param.16) | copy-start | bytes 388
  34.2 14.4 %copy-start.46 = (bf16[1,1,32,8,2,128]{5,4,3,2,1,0:T(2,128)(2,1)S(1)}, bf16[1,1,32,8,2,128]{5,4,3,2,1,0:T(2,128)(2,1)}, u32[]{:S(2)}) copy-start(bf16[1,1,32,8,2,128]{5,4,3,2,1,0:T(2,128)(2,1)} %param.11) | copy-start | bytes 393220
  34.9 7.6 %all-to-all-start.3 = ((bf16[32,8,2,128]{3,0,2,1:T(8,128)(2,1)}), bf16[32,8,2,128]{3,0,2,1:T(8,128)(2,1)S(1)}, u32[]{:S(2)}, u32[]{:S(2)}) async-start(bf16[32,8,2,128]{3,0,2,1:T(8,128)(2,1)} %fusion.39), calls=%async_computation.3 | async-start | bytes 262144 | tf_op jit(solution)/shard_map/all_to_all | solution.py:273
  42.4 13.5 %copy-start.27 = (bf16[1,32,2,8,128]{4,1,0,3,2:T(8,128)(2,1)S(1)}, bf16[1,32,2,8,128]{4,1,0,3,2:T(8,128)(2,1)}, u32[]{:S(2)}) copy-start(bf16[1,32,2,8,128]{4,1,0,3,2:T(8,128)(2,1)} %copy-done.26) | copy-start | bytes 393220
  42.4 13.5 %copy-start.33 = (bf16[1,32,2,8,128]{4,1,0,3,2:T(8,128)(2,1)S(1)}, bf16[1,32,2,8,128]{4,1,0,3,2:T(8,128)(2,1)}, u32[]{:S(2)}) copy-start(bf16[1,32,2,8,128]{4,1,0,3,2:T(8,128)(2,1)} %copy-done.32) | copy-start | bytes 393220
  42.5 13.5 %copy-start.35 = (bf16[1,32,2,8,128]{4,1,0,3,2:T(8,128)(2,1)S(1)}, bf16[1,32,2,8,128]{4,1,0,3,2:T(8,128)(2,1)}, u32[]{:S(2)}) copy-start(bf16[1,32,2,8,128]{4,1,0,3,2:T(8,128)(2,1)} %copy-done.34) | copy-start | bytes 393220
  44.4 7.4 %all-to-all-start.4 = ((f32[4,1,64]{2,1,0:T(1,128)}), f32[4,1,64]{2,1,0:T(1,128)S(1)}, u32[]{:S(2)}, u32[]{:S(2)}) async-start(f32[4,1,64]{2,1,0:T(1,128)} %broadcast_in_dim.20), calls=%async_computation.4 | async-start | bytes 4096 | tf_op jit(solution)/shard_map/all_to_all | solution.py:37
  48.7 7.5 %copy-start.29 = (bf16[1,32,2,8,128]{4,1,3,2,0:T(8,128)(2,1)S(1)}, bf16[1,32,2,8,128]{4,1,3,2,0:T(8,128)(2,1)}, u32[]{:S(2)}) copy-start(bf16[1,32,2,8,128]{4,1,3,2,0:T(8,128)(2,1)} %copy-done.28) | copy-start | bytes 393220
  48.7 7.5 %copy-start.31 = (bf16[1,32,2,8,128]{4,1,3,2,0:T(8,128)(2,1)S(1)}, bf16[1,32,2,8,128]{4,1,3,2,0:T(8,128)(2,1)}, u32[]{:S(2)}) copy-start(bf16[1,32,2,8,128]{4,1,3,2,0:T(8,128)(2,1)} %copy-done.30) | copy-start | bytes 393220
  48.7 7.5 %copy-start.39 = (bf16[1,32,2,8,128]{4,1,3,2,0:T(8,128)(2,1)S(1)}, bf16[1,32,2,8,128]{4,1,3,2,0:T(8,128)(2,1)}, u32[]{:S(2)}) copy-start(bf16[1,32,2,8,128]{4,1,3,2,0:T(8,128)(2,1)} %copy-done.38) | copy-start | bytes 393220
  49.4 16.8 %collective-permute-start.2 = (bf16[1,1,32,2,8,128]{5,2,4,3,1,0:T(8,128)(2,1)S(1)}, bf16[1,1,32,2,8,128]{5,2,4,3,1,0:T(8,128)(2,1)S(1)}, u32[]{:S(2)}, u32[]{:S(2)}) collective-permute-start(bf16[1,1,32,2,8,128]{5,2,4,3,1,0:T(8,128)(2,1)S(1)} %bitcast.781), channel_id=1, source_target_pairs={{0,128},{128,256},{256,384},{1,129},{129,257},{257,385},{2,130},{1... | collective-permute-start | bytes 393224 | tf_op jit(solution)/shard_map/ppermute | solution.py:57
  51.8 8.3 %all-to-all-start.1 = ((bf16[32,2,8,128]{3,0,1,2:T(8,128)(2,1)}), bf16[32,2,8,128]{3,0,1,2:T(8,128)(2,1)S(1)}, u32[]{:S(2)}, u32[]{:S(2)}) async-start(bf16[32,2,8,128]{3,0,1,2:T(8,128)(2,1)} %copy.241), calls=%async_computation.1 | async-start | bytes 262144 | tf_op jit(solution)/shard_map/all_to_all | solution.py:252
  60.1 6.8 %collective-permute-start.3 = (bf16[64,8,1,128]{3,0,2,1:T(8,128)(2,1)S(1)}, bf16[64,8,1,128]{3,0,2,1:T(8,128)(2,1)S(1)}, u32[]{:S(2)}, u32[]{:S(2)}) collective-permute-start(bf16[64,8,1,128]{3,0,2,1:T(8,128)(2,1)S(1)} %get-tuple-element.107), channel_id=1, source_target_pairs={{0,1},{1,2},{2,3},{4,5},{5,6},{6,7},{8,9},{9,10},{10,11},{12,13},{... | collective-permute-start | bytes 393224 | tf_op jit(solution)/shard_map/ppermute | solution.py:26
  63.7 6.3 %collective-permute-start.4 = (bf16[64,8,1,128]{3,0,2,1:T(8,128)(2,1)S(1)}, bf16[64,8,1,128]{3,0,2,1:T(8,128)(2,1)S(1)}, u32[]{:S(2)}, u32[]{:S(2)}) collective-permute-start(bf16[64,8,1,128]{3,0,2,1:T(8,128)(2,1)S(1)} %get-tuple-element.108), channel_id=1, source_target_pairs={{1,0},{2,1},{3,2},{5,4},{6,5},{7,6},{9,8},{10,9},{11,10},{13,12},{... | collective-permute-start | bytes 393224 | tf_op jit(solution)/shard_map/ppermute | solution.py:28
  79.2 5.6 %copy-start.50 = (f32[1,32]{1,0:T(1,128)S(1)}, f32[1,32]{1,0:T(1,128)}, u32[]{:S(2)}) copy-start(f32[1,32]{1,0:T(1,128)} %param.19) | copy-start | bytes 388
  79.9 4.8 %all-to-all-start.2 = ((f32[4,1,64]{2,1,0:T(1,128)}), f32[4,1,64]{2,1,0:T(1,128)S(1)}, u32[]{:S(2)}, u32[]{:S(2)}) async-start(f32[4,1,64]{2,1,0:T(1,128)} %broadcast_in_dim.18), calls=%async_computation.2 | async-start | bytes 4096 | tf_op jit(solution)/shard_map/all_to_all | solution.py:37
  84.9 34.3 %collective-permute-start.5 = (bf16[1,1,32,8,2,128]{5,2,4,3,1,0:T(8,128)(2,1)S(1)}, bf16[1,1,32,8,2,128]{5,2,4,3,1,0:T(8,128)(2,1)S(1)}, u32[]{:S(2)}, u32[]{:S(2)}) collective-permute-start(bf16[1,1,32,8,2,128]{5,2,4,3,1,0:T(8,128)(2,1)S(1)} %fusion.104), channel_id=1, source_target_pairs={{128,0},{256,128},{384,256},{129,1},{257,129},{385,257},{130,2},{2... | collective-permute-start | bytes 393224 | tf_op jit(solution)/shard_map/ppermute | solution.py:57
  (41 other events, 94.6 us)

commit v2 on v0

v2 whole, which is shorter than its diff:
```python
import math

import jax
import jax.numpy as jnp
from jax import lax
from jax.experimental import pallas as pl
from jax.experimental.pallas import tpu as pltpu
from jax.sharding import PartitionSpec as P

SPACE = "space"
DP = "dp"
SECTION = "section"

EPS = 1e-05

C = 32
LANES = 128
FULL = 8
SPLIT = 2
ROWS = FULL * SPLIT
RUN = FULL * LANES
PADDED = (FULL + 2) * LANES
PAIR = SPLIT * LANES
TAPS = 9
WIDE = 3 * C
UNIT = TAPS * WIDE
ORDER = 11
SEND = jnp.bfloat16


def dot(a, b):
    return jnp.dot(a, b, preferred_element_type=jnp.float32)


def dot_t(a, b):
    return lax.dot_general(a, b, (((1,), (1,)), ((), ())), preferred_element_type=jnp.float32)


def lanes_of(shape):
    return lax.broadcasted_iota(jnp.int32, shape, len(shape) - 1)


def to_right(row):
    return jnp.where(lanes_of(row.shape) == 0, 0.0, pltpu.roll(row, 1, 1))


def to_left(row):
    return jnp.where(lanes_of(row.shape) == LANES - 1, 0.0, pltpu.roll(row, LANES - 1, 1))


def gather_taps(row):
    return jnp.concatenate([to_left(row), row, to_right(row)], axis=0).astype(jnp.bfloat16)


def merge_taps(wide):
    return to_right(wide[0:C]) + wide[C : 2 * C] + to_left(wide[2 * C : 3 * C])


def pack_stats(first, second):
    lanes = lanes_of((8, LANES))
    packed = jnp.zeros((8, LANES), jnp.float32)
    for k in range(4):
        for n, whole in enumerate((first, second)):
            part = whole[8 * k : 8 * k + 8]
            for shift in (64, 32, 16):
                part = part + pltpu.roll(part, shift, 1)
            low = 32 * k + 16 * n
            packed = jnp.where((lanes >= low) & (lanes < low + 16), part, packed)
    return packed


def unpack_stats(packed):
    lanes = lanes_of((8, LANES))
    both = []
    for n in range(2):
        pieces = []
        for k in range(4):
            low = 32 * k + 16 * n
            mine = jnp.where((lanes >= low) & (lanes < low + 16), packed, 0.0)
            pieces.append(jnp.sum(mine, axis=1, keepdims=True))
        both.append(jnp.concatenate(pieces, axis=0))
    return both


def kernel(
    n_section, n_dp, n_space, voxels, grad_scale,
    enc_in, dec_in, cot_in, deep_in, enc_w, dec_w, enc_gain, enc_bias, dec_gain, dec_bias,
    enc_out, dec_out, total,
    stage, back, x, xd, xs, cot, cot_halo, c3, e3, skip_send, sg, gr, deep, pre, dec_pre,
    prm, tr_w, stat_send, stat_got, grads, terms, arrived, near_send, near_got,
    enc_flat, dec_flat,
    halo_s, halo_r, stat_s, stat_r, skip_s, skip_r, sg_s, sg_r, own_sem,
    hand_s, hand_r, far_s, far_r, near_s, near_r,
):
    me = lax.axis_index(DP)
    slab = lax.axis_index(SPACE)
    level = lax.axis_index(SECTION)
    last = n_space - 1
    barrier = pltpu.get_barrier_semaphore()

    def greet(i, carry):
        pl.semaphore_signal(barrier, inc=1, device_id={DP: lax.rem(me + i, n_dp)})
        return carry

    for i in range(1, n_space):
        pl.semaphore_signal(barrier, inc=1, device_id={SPACE: lax.rem(slab + i, n_space)})
    lax.fori_loop(1, n_dp, greet, 0)

    @pl.when(level > 0)
    def _():
        pl.semaphore_signal(barrier, inc=1, device_id={SECTION: level - 1})

    @pl.when(level < n_section - 1)
    def _():
        pl.semaphore_signal(barrier, inc=1, device_id={SECTION: level + 1})

    stage[0] = enc_in[...].astype(jnp.float32)
    stage[1] = cot_in[...].astype(jnp.float32)
    stage[2] = dec_in[...].astype(jnp.float32)
    stage[3] = deep_in[...].astype(jnp.float32)

    def row_of(k, r):
        return stage[k, pl.ds(r, C, stride=ROWS), :]

    for ref in (x, xd, xs):
        ref[:, :, 0:LANES] = jnp.zeros((4, C, LANES), ref.dtype)
        ref[:, :, PADDED - LANES : PADDED] = jnp.zeros((4, C, LANES), ref.dtype)
    c3[:, :, 0:LANES] = jnp.zeros((4, WIDE, LANES), c3.dtype)
    c3[:, :, PADDED - LANES : PADDED] = jnp.zeros((4, WIDE, LANES), c3.dtype)
    for u in range(SPLIT):
        for v in range(FULL):
            at = slice((1 + v) * LANES, (2 + v) * LANES)
            x[1 + u, :, at] = row_of(0, u * FULL + v).astype(jnp.bfloat16)
            cot[u, :, v * LANES : (v + 1) * LANES] = row_of(1, v * SPLIT + u).astype(jnp.bfloat16)
            xd[1 + u, :, at] = row_of(2, v * SPLIT + u).astype(jnp.bfloat16)

    @pl.when(slab == 0)
    def _():
        x[0] = jnp.zeros((C, PADDED), x.dtype)
        xd[0] = jnp.zeros((C, PADDED), xd.dtype)
        cot_halo[0] = jnp.zeros((C, RUN), cot_halo.dtype)

    @pl.when(slab == last)
    def _():
        x[3] = jnp.zeros((C, PADDED), x.dtype)
        xd[3] = jnp.zeros((C, PADDED), xd.dtype)
        cot_halo[1] = jnp.zeros((C, RUN), cot_halo.dtype)

    inner = slice(LANES, LANES + RUN)

    def halo(k, up):
        src_u, dst_u, peer = (2, 0, slab + 1) if up else (1, 3, slab - 1)
        if k == 1:
            src, dst = cot.at[src_u - 1], cot_halo.at[0 if up else 1]
        else:
            ref = x if k == 0 else xd
            src, dst = ref.at[src_u, :, inner], ref.at[dst_u, :, inner]
        n = 2 * k + (0 if up else 1)
        return pltpu.make_async_remote_copy(
            src_ref=src, dst_ref=dst, send_sem=halo_s.at[n], recv_sem=halo_r.at[n],
            device_id={SPACE: peer},
        )

    pl.semaphore_wait(
        barrier, n_dp + n_space - 2 + lax.min(level, 1) + lax.min(n_section - 1 - level, 1)
    )

    @pl.when(slab < last)
    def _():
        for k in range(3):
            halo(k, True).start()

    @pl.when(slab > 0)
    def _():
        for k in range(3):
            halo(k, False).start()

    def halo_arrived(k):
        @pl.when(slab > 0)
        def _():
            halo(k, True).wait_recv()

        @pl.when(slab < last)
        def _():
            halo(k, False).wait_recv()

    zeros_row = jnp.zeros((LANES, LANES), jnp.float32)
    prm[...] = zeros_row
    prm[0:1, 0:C] = enc_gain[...]
    prm[1:2, 0:C] = enc_bias[...]
    prm[2:3, 0:C] = dec_gain[...]
    prm[3:4, 0:C] = dec_bias[...]
    columns = prm[...].T
    e_gain, e_bias = columns[0:C, 0:1], columns[0:C, 1:2]
    d_gain, d_bias = columns[0:C, 2:3], columns[0:C, 3:4]
    pick = (
        lax.broadcasted_iota(jnp.int32, (C, 2 * C), 1)
        == lax.broadcasted_iota(jnp.int32, (C, 2 * C), 0) + C
    ).astype(jnp.bfloat16)
    for t in range(TAPS):
        tr_w[t] = dot_t(pick, dec_w[t]).astype(jnp.bfloat16)
    for u in range(SPLIT):
        for v in range(FULL):
            c3[1 + u, :, (1 + v) * LANES : (2 + v) * LANES] = gather_taps(row_of(1, v * SPLIT + u))
            deep[v, :, u * LANES : (u + 1) * LANES] = row_of(3, u * FULL + v)

    zero = jnp.zeros((C, LANES), jnp.float32)
    chunk = 2

    halo_arrived(0)
    first, second = zero, zero
    for u in range(SPLIT):
        for q in range(0, FULL, chunk):
            acc = jnp.zeros((WIDE, chunk * LANES), jnp.float32)
            for a in range(3):
                for b in range(3):
                    at = (q + b) * LANES
                    acc = acc + dot(enc_w[3 * a + b], x[u + a, :, at : at + chunk * LANES])
            for r in range(chunk):
                row = merge_taps(acc[:, r * LANES : (r + 1) * LANES])
                pre[q + r, :, u * LANES : (u + 1) * LANES] = row
                first = first + row
                second = second + row * row

    def stat_copy(n, i):
        k = n * (n_space - 1) + i - 1
        return pltpu.make_async_remote_copy(
            src_ref=stat_send.at[n], dst_ref=stat_got.at[k],
            send_sem=stat_s.at[k], recv_sem=stat_r.at[k],
            device_id={SPACE: lax.rem(slab + i, n_space)},
        )

    def send_stats(n, first, second):
        stat_send[n] = pack_stats(first, second)
        for i in range(1, n_space):
            stat_copy(n, i).start()

    def all_stats(n):
        packed = stat_send[n]
        for i in range(1, n_space):
            stat_copy(n, i).wait_recv()
            packed = packed + stat_got[n * (n_space - 1) + i - 1]
        one, two = unpack_stats(packed)
        return one * (1.0 / voxels), two * (1.0 / voxels)

    send_stats(0, first, second)

    halo_arrived(1)
    for side, u in ((0, 0), (1, 3)):
        for v in range(FULL):
            row = cot_halo[side, :, v * LANES : (v + 1) * LANES].astype(jnp.float32)
            c3[u, :, (1 + v) * LANES : (2 + v) * LANES] = gather_taps(row)
    for u in range(SPLIT):
        for q in range(0, FULL, chunk):
            acc = jnp.zeros((C, chunk * LANES), jnp.float32)
            for a in range(3):
                for b in range(3):
                    at = (q + 2 - a) * LANES
                    acc = acc + dot(tr_w[3 * a + b], c3[u + 2 - b, :, at : at + chunk * LANES])
            sg[u, :, q * LANES : (q + chunk) * LANES] = acc.astype(jnp.bfloat16)

    def sg_copy(i):
        peer = lax.rem(slab + i, n_space)
        return pltpu.make_async_remote_copy(
            src_ref=sg.at[:, :, pl.ds(pl.multiple_of(peer * PAIR, LANES), PAIR)],
            dst_ref=gr.at[pl.ds(slab * SPLIT, SPLIT)],
            send_sem=sg_s.at[i - 1], recv_sem=sg_r.at[i - 1], device_id={SPACE: peer},
        )

    def sg_arrival(i):
        peer = lax.rem(slab - i + n_space, n_space)
        return pltpu.make_async_remote_copy(
            src_ref=sg.at[:, :, pl.ds(pl.multiple_of(peer * PAIR, LANES), PAIR)],
            dst_ref=gr.at[pl.ds(peer * SPLIT, SPLIT)],
            send_sem=sg_s.at[i - 1], recv_sem=sg_r.at[i - 1], device_id={SPACE: peer},
        )

    sg_own = pltpu.make_async_copy(
        sg.at[:, :, pl.ds(pl.multiple_of(slab * PAIR, LANES), PAIR)],
        gr.at[pl.ds(slab * SPLIT, SPLIT)],
        own_sem.at[0],
    )
    for i in range(1, n_space):
        sg_copy(i).start()
    sg_own.start()

    e_mean, e_square = all_stats(0)
    e_scale = lax.rsqrt(e_square - e_mean * e_mean + EPS)

    def enc_hat_of(v, u):
        return (pre[v, :, u * LANES : (u + 1) * LANES] - e_mean) * e_scale

    skip_send[0] = jnp.zeros((C, PAIR), jnp.bfloat16)
    skip_send[FULL + 1] = jnp.zeros((C, PAIR), jnp.bfloat16)
    for v in range(FULL):
        for u in range(SPLIT):
            act = jnp.maximum(e_gain * enc_hat_of(v, u) + e_bias, 0.0).astype(jnp.bfloat16)
            skip_send[1 + v, :, u * LANES : (u + 1) * LANES] = act
            back[0, pl.ds(u * FULL + v, C, stride=ROWS), :] = act.astype(jnp.float32)

    def skip_refs(source, target):
        return (
            skip_send.at[pl.ds(target * SPLIT, SPLIT + 2)],
            xs.at[:, :, pl.ds(pl.multiple_of((1 + source * SPLIT) * LANES, LANES), PAIR)],
        )

    def skip_copy(i):
        peer = lax.rem(slab + i, n_space)
        src, dst = skip_refs(slab, peer)
        return pltpu.make_async_remote_copy(
            src_ref=src, dst_ref=dst, send_sem=skip_s.at[i - 1], recv_sem=skip_r.at[i - 1],
            device_id={SPACE: peer},
        )

    def skip_arrival(i):
        peer = lax.rem(slab - i + n_space, n_space)
        src, dst = skip_refs(peer, slab)
        return pltpu.make_async_remote_copy(
            src_ref=src, dst_ref=dst, send_sem=skip_s.at[i - 1], recv_sem=skip_r.at[i - 1],
            device_id={SPACE: peer},
        )

    skip_own = pltpu.make_async_copy(*skip_refs(slab, slab), own_sem.at[1])
    for i in range(1, n_space):
        skip_copy(i).start()
    skip_own.start()
    enc_flat[...] = back[0].astype(jnp.bfloat16)

    for i in range(1, n_space):
        sg_arrival(i).wait_recv()
    sg_own.wait()

    def gated_of(v, u, hat):
        at = slice(u * LANES, (u + 1) * LANES)
        upstream = gr[v, :, at].astype(jnp.float32) + deep[v, :, at]
        return jnp.where(e_gain * hat + e_bias > 0, upstream, 0.0) * e_gain

    first, second = zero, zero
    for v in range(FULL):
        for u in range(SPLIT):
            hat = enc_hat_of(v, u)
            gated = gated_of(v, u, hat)
            first = first + gated
            second = second + gated * hat
    send_stats(1, first, second)

    lanes8 = lanes_of((8, LANES))
    per_peer = UNIT // n_dp
    group = -(-per_peer // 4)

    def send_unit(n, left, right):
        for a in range(3):
            for b in range(3):
                acc = jnp.zeros((WIDE, C), jnp.float32)
                for u in range(SPLIT):
                    acc = acc + dot_t(left(u), right(u, a, b))
                t = 3 * a + b
                grads[n, t * WIDE : (t + 1) * WIDE, 0:C] = acc * grad_scale
        for p in range(n_dp):
            block = grads[n, p * per_peer : p * per_peer + 8, :]
            for g in range(1, 4):
                at = p * per_peer + g * group
                moved = pltpu.roll(grads[n, at : at + 8, :], 32 * g, 1)
                block = jnp.where(lanes8 < 32 * g, block, moved)
            terms[n, p] = block.astype(SEND)

        def start(i, carry):
            far_copy(n, i).start()
            return carry

        lax.fori_loop(1, n_dp, start, 0)

    def far_copy(n, i):
        peer = lax.rem(me + i * ORDER, n_dp)
        return pltpu.make_async_remote_copy(
            src_ref=terms.at[n, peer], dst_ref=arrived.at[n, me],
            send_sem=far_s.at[n, peer], recv_sem=far_r.at[n, me], device_id={DP: peer},
        )

    def far_arrival(n, i):
        peer = lax.rem(me - i * ORDER + n_dp * ORDER, n_dp)
        return peer, pltpu.make_async_remote_copy(
            src_ref=terms.at[n, peer], dst_ref=arrived.at[n, peer],
            send_sem=far_s.at[n, peer], recv_sem=far_r.at[n, peer], device_id={DP: peer},
        )

    halo_arrived(2)
    send_unit(
        1,
        lambda u: c3[1 + u, :, inner],
        lambda u, a, b: xd[u + b, :, a * LANES : a * LANES + RUN],
    )

    for i in range(1, n_space):
        skip_arrival(i).wait_recv()
    skip_own.wait()
    first, second = zero, zero
    for u in range(SPLIT):
        for q in range(0, FULL, chunk):
            acc = jnp.zeros((WIDE, chunk * LANES), jnp.float32)
            for a in range(3):
                for b in range(3):
                    at = slice((q + a) * LANES, (q + a + chunk) * LANES)
                    joined = jnp.concatenate([xd[u + b, :, at], xs[u + b, :, at]], axis=0)
                    acc = acc + dot(dec_w[3 * a + b], joined)
            for r in range(chunk):
                row = merge_taps(acc[:, r * LANES : (r + 1) * LANES])
                dec_pre[u, :, (q + r) * LANES : (q + r + 1) * LANES] = row
                first = first + row
                second = second + row * row
    send_stats(2, first, second)

    def hand(k):
        src, dst, step = (enc_flat, enc_out, 1) if k == 0 else (dec_flat, dec_out, -1)
        return pltpu.make_async_remote_copy(
            src_ref=src, dst_ref=dst, send_sem=hand_s.at[k], recv_sem=hand_r.at[k],
            device_id={SECTION: level + step},
        )

    @pl.when(level < n_section - 1)
    def _():
        hand(0).start()

    g_mean, gh_mean = all_stats(1)
    for u in range(SPLIT):
        for v in range(FULL):
            hat = enc_hat_of(v, u)
            row = (gated_of(v, u, hat) - g_mean - hat * gh_mean) * e_scale
            row = row.astype(jnp.bfloat16).astype(jnp.float32)
            e3[u, :, v * LANES : (v + 1) * LANES] = gather_taps(row)
    send_unit(
        0,
        lambda u: e3[u],
        lambda u, a, b: x[u + a, :, b * LANES : b * LANES + RUN],
    )
    send_unit(
        2,
        lambda u: c3[1 + u, :, inner],
        lambda u, a, b: xs[u + b, :, a * LANES : a * LANES + RUN],
    )

    d_mean, d_square = all_stats(2)
    d_scale = lax.rsqrt(d_square - d_mean * d_mean + EPS)
    for u in range(SPLIT):
        for v in range(FULL):
            hat = (dec_pre[u, :, v * LANES : (v + 1) * LANES] - d_mean) * d_scale
            back[1, pl.ds(v * SPLIT + u, C, stride=ROWS), :] = jnp.maximum(
                d_gain * hat + d_bias, 0.0
            )
    dec_flat[...] = back[1].astype(jnp.bfloat16)

    @pl.when(level > 0)
    def _():
        hand(1).start()

    @pl.when(level == 0)
    def _():
        enc_out[...] = jnp.zeros(enc_out.shape, enc_out.dtype)

    @pl.when(level == n_section - 1)
    def _():
        dec_out[...] = jnp.zeros(dec_out.shape, dec_out.dtype)

    for n in range(3):
        def collect(i, acc):
            peer, copy = far_arrival(n, i)
            copy.wait_recv()
            return acc + arrived[n, peer].astype(jnp.float32)

        near_send[n] = lax.fori_loop(1, n_dp, collect, terms[n, me].astype(jnp.float32))

    def near_copy(i):
        return pltpu.make_async_remote_copy(
            src_ref=near_send, dst_ref=near_got.at[i - 1],
            send_sem=near_s.at[i - 1], recv_sem=near_r.at[i - 1],
            device_id={SPACE: lax.rem(slab + i, n_space)},
        )

    for i in range(1, n_space):
        near_copy(i).start()
    acc = near_send[...]
    for i in range(1, n_space):
        near_copy(i).wait_recv()
        acc = acc + near_got[i - 1]
    total[...] = acc

    @pl.when(level > 0)
    def _():
        hand(0).wait_recv()
        hand(1).wait_send()

    @pl.when(level < n_section - 1)
    def _():
        hand(1).wait_recv()
        hand(0).wait_send()

    @pl.when(slab < last)
    def _():
        for k in range(3):
            halo(k, True).wait_send()

    @pl.when(slab > 0)
    def _():
        for k in range(3):
            halo(k, False).wait_send()

    for i in range(1, n_space):
        for n in range(3):
            stat_copy(n, i).wait_send()
        sg_copy(i).wait_send()
        skip_copy(i).wait_send()
        near_copy(i).wait_send()
    for n in range(3):
        def drain(i, carry):
            far_copy(n, i).wait_send()
            return carry

        lax.fori_loop(1, n_dp, drain, 0)


def body(
    enc_input, dec_input, dec_cotangent, deep_cotangent,
    enc_weight, dec_weight, enc_gain, enc_bias, dec_gain, dec_bias,
):
    n_section, n_dp, n_space = (lax.axis_size(a) for a in (SECTION, DP, SPACE))
    voxels = enc_input.shape[3] * n_space * enc_input.shape[4] * enc_input.shape[5]
    grad_scale = 1.0 / math.sqrt(n_dp * voxels)
    flat = (C * ROWS, LANES)
    vmem = pl.BlockSpec(memory_space=pltpu.VMEM)
    bf16, f32 = jnp.bfloat16, jnp.float32
    dma = pltpu.SemaphoreType.DMA
    others = n_space - 1
    enc_out, dec_out, total = pl.pallas_call(
        lambda *refs: kernel(n_section, n_dp, n_space, voxels, grad_scale, *refs),
        out_shape=(
            jax.ShapeDtypeStruct(flat, bf16),
            jax.ShapeDtypeStruct(flat, bf16),
            jax.ShapeDtypeStruct((3, 8, LANES), f32),
        ),
        in_specs=[vmem] * 10,
        out_specs=(vmem, vmem, vmem),
        scratch_shapes=[
            pltpu.VMEM((4, *flat), f32),
            pltpu.VMEM((2, *flat), f32),
            pltpu.VMEM((4, C, PADDED), bf16),
            pltpu.VMEM((4, C, PADDED), bf16),
            pltpu.VMEM((4, C, PADDED), bf16),
            pltpu.VMEM((SPLIT, C, RUN), bf16),
            pltpu.VMEM((2, C, RUN), bf16),
            pltpu.VMEM((4, WIDE, PADDED), bf16),
            pltpu.VMEM((SPLIT, WIDE, RUN), bf16),
            pltpu.VMEM((FULL + 2, C, PAIR), bf16),
            pltpu.VMEM((SPLIT, C, RUN), bf16),
            pltpu.VMEM((FULL, C, PAIR), bf16),
            pltpu.VMEM((FULL, C, PAIR), f32),
            pltpu.VMEM((FULL, C, PAIR), f32),
            pltpu.VMEM((SPLIT, C, RUN), f32),
            pltpu.VMEM((LANES, LANES), f32),
            pltpu.VMEM((TAPS, C, WIDE), bf16),
            pltpu.VMEM((3, 8, LANES), f32),
            pltpu.VMEM((3 * others, 8, LANES), f32),
            pltpu.VMEM((3, UNIT + 8, LANES), f32),
            pltpu.VMEM((3, n_dp, 8, LANES), SEND),
            pltpu.VMEM((3, n_dp, 8, LANES), SEND),
            pltpu.VMEM((3, 8, LANES), f32),
            pltpu.VMEM((others, 3, 8, LANES), f32),
            pltpu.VMEM(flat, bf16),
            pltpu.VMEM(flat, bf16),
            dma((6,)), dma((6,)),
            dma((3 * others,)), dma((3 * others,)),
            dma((others,)), dma((others,)),
            dma((others,)), dma((others,)),
            dma((2,)),
            dma((2,)), dma((2,)),
            dma((3, n_dp)), dma((3, n_dp)),
            dma((others,)), dma((others,)),
        ],
        compiler_params=pltpu.CompilerParams(
            collective_id=0, has_side_effects=True, vmem_limit_bytes=48 * 1024 * 1024
        ),
    )(
        enc_input.reshape(flat), dec_input.reshape(flat), dec_cotangent.reshape(flat),
        deep_cotangent.reshape(flat), enc_weight.reshape(TAPS, WIDE, C),
        dec_weight.reshape(TAPS, WIDE, 2 * C), enc_gain, enc_bias, dec_gain, dec_bias,
    )
    per_peer = UNIT // n_dp
    group = -(-per_peer // 4)
    units = total[:, :group].reshape(3, group, 4, C).transpose(0, 2, 1, 3)
    units = units.reshape(3, 4 * group, C)[:, :per_peer]
    slab = lax.axis_index(SPACE)
    enc_sums = units[0].reshape(n_space, -1)
    dec_sums = jnp.concatenate([units[1], units[2]], axis=1).reshape(n_space, -1)
    return (
        enc_out.reshape(enc_input.shape),
        dec_out.reshape(dec_input.shape),
        lax.dynamic_index_in_dim(enc_sums, slab, 0),
        lax.dynamic_index_in_dim(dec_sums, slab, 0),
    )


def solution(mesh):
    by_depth = P(SECTION, DP, None, SPACE, None, None)
    by_height = P(SECTION, DP, None, None, SPACE, None)
    whole3, whole1 = P(SECTION, None, None, None), P(SECTION, None)
    return jax.shard_map(
        body,
        mesh=mesh,
        in_specs=(by_depth, by_height, by_height, by_depth, whole3, whole3, *[whole1] * 4),
        out_specs=(by_depth, by_height, P(SECTION, (DP, SPACE)), P(SECTION, (DP, SPACE))),
        check_vma=False,
    )
```

time: 139 us -> 52.8 us (0.38)
  the two profiles are of different devices: /device:TPU:16 before, /device:TPU:1 now
where the time goes in v2:
time: 52.8 us; the launch traced here: 52.6 us
  Pallas kernels  42.9 us (81%)
  local copies, waits for them, and re-layouts  8.9 us (17%)
  between operations  0.72 us (1%)
    pallas_call x1, Pallas kernels, body(): pl.pallas_call(lambda *refs: kernel(n_section, n_dp, n_space, voxels, gra...  42.9 us
    unnamed x22, local copies, waits for them, and re-layouts  7.47 us

profile of v2, /device:TPU:1, one launch (start us, length us, event | category | flops | bytes accessed | tf_op | source)
XLA Modules:
  0.0 52.6 jit_solution(2101508941706931871)
XLA Ops:
  0.6 0.0 copy-start.9
  0.6 0.0 copy-start.6
  0.7 0.0 copy-start.7
  0.7 0.0 copy-start.8
  0.7 0.6 %copy-done.9 = f32[1,32]{1,0:T(1,128)S(1)} copy-done((f32[1,32]{1,0:T(1,128)S(1)}, f32[1,32]{1,0:T(1,128)}, u32[]{:S(2)}) %copy-start.9) | copy-done | bytes 152
  1.3 0.0 copy-done.6
  1.3 0.0 copy-done.7
  1.3 0.0 copy-done.8
  1.3 0.0 copy-start
  1.3 0.9 %copy-done = bf16[1,27,32,32]{3,2,1,0:T(8,128)(2,1)S(1)} copy-done((bf16[1,27,32,32]{3,2,1,0:T(8,128)(2,1)S(1)}, bf16[1,27,32,32]{3,2,1,0:T(8,128)(2,1)}, u32[]{:S(2)}) %copy-start) | copy-done | bytes 55320
  2.3 0.9 %copy-done.1 = bf16[1,27,32,64]{3,2,1,0:T(8,128)(2,1)S(1)} copy-done((bf16[1,27,32,64]{3,2,1,0:T(8,128)(2,1)S(1)}, bf16[1,27,32,64]{3,2,1,0:T(8,128)(2,1)}, u32[]{:S(2)}) %copy-start.1) | copy-done | bytes 110616
  3.2 0.9 %copy-done.2 = bf16[1,1,32,2,8,128]{5,4,3,2,1,0:T(8,128)(2,1)S(1)} copy-done((bf16[1,1,32,2,8,128]{5,4,3,2,1,0:T(8,128)(2,1)S(1)}, bf16[1,1,32,2,8,128]{5,4,3,2,1,0:T(8,128)(2,1)}, u32[]{:S(2)}) %copy-start.2) | copy-done | bytes 131096
  4.1 0.9 %copy-done.3 = bf16[1,1,32,8,2,128]{5,4,3,2,1,0:T(2,128)(2,1)S(1)} copy-done((bf16[1,1,32,8,2,128]{5,4,3,2,1,0:T(2,128)(2,1)S(1)}, bf16[1,1,32,8,2,128]{5,4,3,2,1,0:T(2,128)(2,1)}, u32[]{:S(2)}) %copy-start.3) | copy-done | bytes 131096
  5.0 0.9 %copy-done.4 = bf16[1,1,32,8,2,128]{5,4,3,2,1,0:T(2,128)(2,1)S(1)} copy-done((bf16[1,1,32,8,2,128]{5,4,3,2,1,0:T(2,128)(2,1)S(1)}, bf16[1,1,32,8,2,128]{5,4,3,2,1,0:T(2,128)(2,1)}, u32[]{:S(2)}) %copy-start.4) | copy-done | bytes 131096
  5.9 0.9 %copy-done.5 = bf16[1,1,32,2,8,128]{5,4,3,2,1,0:T(8,128)(2,1)S(1)} copy-done((bf16[1,1,32,2,8,128]{5,4,3,2,1,0:T(8,128)(2,1)S(1)}, bf16[1,1,32,2,8,128]{5,4,3,2,1,0:T(8,128)(2,1)}, u32[]{:S(2)}) %copy-start.5) | copy-done | bytes 131096
  6.8 42.9 %shard_map.129 = (bf16[512,128]{1,0:T(8,128)(2,1)S(1)}, bf16[512,128]{1,0:T(8,128)(2,1)S(1)}, f32[3,8,128]{2,1,0:T(8,128)S(1)}) custom-call(bf16[512,128]{1,0:T(8,128)(2,1)S(1)} %bitcast.20, bf16[512,128]{1,0:T(8,128)(2,1)S(1)} %bitcast.21, bf16[512,128]{1,0:T(8,128)(2,1)S(1)} %bitcast.22, bf16[512,128]{1,0:T(8,128)(2,1)S(1)} %bitcast.23, ...), custom_call_target="tpu_custom_call" | custom-call | tf_op jit(solution)/shard_map/pallas_call | solution.py:533
  49.7 0.1 reshape.49
  49.8 0.1 pad_maximum_fusion
  49.9 0.1 reshape.51
  50.0 0.6 %constant_dynamic-slice_fusion = f32[1,432]{1,0:T(1,128)} fusion(f32[4,432]{1,0:T(4,128)S(1)} %reshape.51, s32[]{:T(128)S(6)} %select_n.6), kind=kLoop, calls=%fused_computation.4 | loop fusion | bytes 3460 | tf_op jit(solution)/shard_map/jit(dynamic_index_in_dim)/dynamic_slice | solution.py:597
  50.6 0.1 reshape_squeeze.3
  50.7 0.6 %constant_dynamic-slice_fusion.1 = f32[1,216]{1,0:T(1,128)} fusion(f32[4,216]{1,0:T(4,128)S(1)} %reshape_squeeze.3, s32[]{:T(128)S(6)} %select_n.6), kind=kLoop, calls=%fused_computation.5 | loop fusion | bytes 1732 | tf_op jit(solution)/shard_map/jit(dynamic_index_in_dim)/dynamic_slice | solution.py:596
  51.3 0.7 %copy.19 = bf16[1,1,32,2,8,128]{5,4,3,2,1,0:T(8,128)(2,1)} copy(bf16[1,1,32,2,8,128]{5,4,3,2,1,0:T(8,128)(2,1)S(1)} %bitcast.19) | data formatting | bytes 262144
  51.9 0.7 %copy.20 = bf16[1,1,32,8,2,128]{5,4,3,2,1,0:T(2,128)(2,1)} copy(bf16[1,1,32,8,2,128]{5,4,3,2,1,0:T(2,128)(2,1)S(1)} %bitcast.18) | data formatting | bytes 262144
  (8 shorter events, 0.0 us)
Async XLA Ops:
  0.6 0.7 %copy-start.9 = (f32[1,32]{1,0:T(1,128)S(1)}, f32[1,32]{1,0:T(1,128)}, u32[]{:S(2)}) copy-start(f32[1,32]{1,0:T(1,128)} %refs_9_.1) | copy-start | bytes 388
  0.6 0.7 %copy-start.6 = (f32[1,32]{1,0:T(1,128)S(1)}, f32[1,32]{1,0:T(1,128)}, u32[]{:S(2)}) copy-start(f32[1,32]{1,0:T(1,128)} %refs_6_.1) | copy-start | bytes 388
  0.7 0.7 %copy-start.7 = (f32[1,32]{1,0:T(1,128)S(1)}, f32[1,32]{1,0:T(1,128)}, u32[]{:S(2)}) copy-start(f32[1,32]{1,0:T(1,128)} %refs_7_.1) | copy-start | bytes 388
  0.7 0.7 %copy-start.8 = (f32[1,32]{1,0:T(1,128)S(1)}, f32[1,32]{1,0:T(1,128)}, u32[]{:S(2)}) copy-start(f32[1,32]{1,0:T(1,128)} %refs_8_.1) | copy-start | bytes 388
  1.3 0.9 %copy-start = (bf16[1,27,32,32]{3,2,1,0:T(8,128)(2,1)S(1)}, bf16[1,27,32,32]{3,2,1,0:T(8,128)(2,1)}, u32[]{:S(2)}) copy-start(bf16[1,27,32,32]{3,2,1,0:T(8,128)(2,1)} %param.14) | copy-start | bytes 165892
  2.3 0.9 %copy-start.1 = (bf16[1,27,32,64]{3,2,1,0:T(8,128)(2,1)S(1)}, bf16[1,27,32,64]{3,2,1,0:T(8,128)(2,1)}, u32[]{:S(2)}) copy-start(bf16[1,27,32,64]{3,2,1,0:T(8,128)(2,1)} %param.15) | copy-start | bytes 331780
  3.2 0.9 %copy-start.2 = (bf16[1,1,32,2,8,128]{5,4,3,2,1,0:T(8,128)(2,1)S(1)}, bf16[1,1,32,2,8,128]{5,4,3,2,1,0:T(8,128)(2,1)}, u32[]{:S(2)}) copy-start(bf16[1,1,32,2,8,128]{5,4,3,2,1,0:T(8,128)(2,1)} %param.10) | copy-start | bytes 393220
  4.1 0.9 %copy-start.3 = (bf16[1,1,32,8,2,128]{5,4,3,2,1,0:T(2,128)(2,1)S(1)}, bf16[1,1,32,8,2,128]{5,4,3,2,1,0:T(2,128)(2,1)}, u32[]{:S(2)}) copy-start(bf16[1,1,32,8,2,128]{5,4,3,2,1,0:T(2,128)(2,1)} %param.11) | copy-start | bytes 393220
  5.0 0.9 %copy-start.4 = (bf16[1,1,32,8,2,128]{5,4,3,2,1,0:T(2,128)(2,1)S(1)}, bf16[1,1,32,8,2,128]{5,4,3,2,1,0:T(2,128)(2,1)}, u32[]{:S(2)}) copy-start(bf16[1,1,32,8,2,128]{5,4,3,2,1,0:T(2,128)(2,1)} %param.12) | copy-start | bytes 393220
  5.9 0.9 %copy-start.5 = (bf16[1,1,32,2,8,128]{5,4,3,2,1,0:T(8,128)(2,1)S(1)}, bf16[1,1,32,2,8,128]{5,4,3,2,1,0:T(8,128)(2,1)}, u32[]{:S(2)}) copy-start(bf16[1,1,32,2,8,128]{5,4,3,2,1,0:T(8,128)(2,1)} %param.13) | copy-start | bytes 393220

commit v3 on v2

v3 whole, which is shorter than its diff:
```python
import math

import jax
import jax.numpy as jnp
from jax import lax
from jax.experimental import pallas as pl
from jax.experimental.pallas import tpu as pltpu
from jax.sharding import PartitionSpec as P

SPACE = "space"
DP = "dp"
SECTION = "section"

EPS = 1e-05

C = 32
LANES = 128
FULL = 8
SPLIT = 2
ROWS = FULL * SPLIT
RUN = FULL * LANES
PADDED = (FULL + 2) * LANES
PAIR = SPLIT * LANES
TAPS = 9
WIDE = 3 * C
UNIT = TAPS * WIDE
ORDER = 11
SEND = jnp.bfloat16


def dot(a, b):
    return jnp.dot(a, b, preferred_element_type=jnp.float32)


def dot_t(a, b):
    return lax.dot_general(a, b, (((1,), (1,)), ((), ())), preferred_element_type=jnp.float32)


def lanes_of(shape):
    return lax.broadcasted_iota(jnp.int32, shape, len(shape) - 1)


def to_right(row):
    return jnp.where(lanes_of(row.shape) == 0, 0.0, pltpu.roll(row, 1, 1))


def to_left(row):
    return jnp.where(lanes_of(row.shape) == LANES - 1, 0.0, pltpu.roll(row, LANES - 1, 1))


def gather_taps(row):
    return jnp.concatenate([to_left(row), row, to_right(row)], axis=0).astype(jnp.bfloat16)


def merge_taps(wide):
    return to_right(wide[0:C]) + wide[C : 2 * C] + to_left(wide[2 * C : 3 * C])


def pack_stats(first, second):
    lanes = lanes_of((8, LANES))
    packed = jnp.zeros((8, LANES), jnp.float32)
    for k in range(4):
        for n, whole in enumerate((first, second)):
            part = whole[8 * k : 8 * k + 8]
            for shift in (64, 32, 16):
                part = part + pltpu.roll(part, shift, 1)
            low = 32 * k + 16 * n
            packed = jnp.where((lanes >= low) & (lanes < low + 16), part, packed)
    return packed


def pack_pair(first, second):
    lanes = lanes_of((8, LANES))
    packed = jnp.zeros((8, LANES), jnp.float32)
    for k in range(4):
        for n, whole in enumerate((first, second)):
            low = 32 * k + 16 * n
            mine = (lanes >= low) & (lanes < low + 16)
            packed = jnp.where(mine, whole[8 * k : 8 * k + 8], packed)
    return packed


def unpack(packed, width):
    lanes = lanes_of((8, LANES))
    both = []
    for n in range(2):
        pieces = []
        for k in range(4):
            low = 32 * k + 16 * n
            mine = jnp.where((lanes >= low) & (lanes < low + width), packed, 0.0)
            pieces.append(jnp.sum(mine, axis=1, keepdims=True))
        both.append(jnp.concatenate(pieces, axis=0))
    return both


def kernel(
    n_section, n_dp, n_space, voxels, grad_scale,
    enc_hbm, dec_hbm, cot_hbm, deep_hbm, enc_w_hbm, dec_w_hbm, g0, g1, g2, g3,
    enc_out, dec_out, total,
    loaded, enc_w, dec_w, params,
    stage, back, x, xd, xs, xc, cot_send, c3, c3e, e3, skip_send, sg, deep, pre, dec_pre,
    prm, tr_w, stat_send, stat_got, grads, terms, arrived, near_send, near_got,
    enc_flat, dec_raw, dec_got, coef_send, coef_got,
    load_s, halo_s, halo_r, stat_s, stat_r, skip_s, skip_r, cot_s, cot_r, own_sem,
    hand_s, hand_r, far_s, far_r, near_s, near_r,
):
    me = lax.axis_index(DP)
    slab = lax.axis_index(SPACE)
    level = lax.axis_index(SECTION)
    last = n_space - 1
    cells = ROWS * LANES

    loads = [
        pltpu.make_async_copy(src, dst, load_s.at[n])
        for n, (src, dst) in enumerate(
            (
                (enc_hbm, loaded.at[0]), (cot_hbm, loaded.at[1]), (enc_w_hbm, enc_w),
                (dec_hbm, loaded.at[2]), (deep_hbm, loaded.at[3]), (dec_w_hbm, dec_w),
                (g0, params.at[0]), (g1, params.at[1]), (g2, params.at[2]), (g3, params.at[3]),
            )
        )
    ]
    for load in loads:
        load.start()

    barrier = pltpu.get_barrier_semaphore()

    def greet(i, carry):
        pl.semaphore_signal(barrier, inc=1, device_id={DP: lax.rem(me + i, n_dp)})
        return carry

    for i in range(1, n_space):
        pl.semaphore_signal(barrier, inc=1, device_id={SPACE: lax.rem(slab + i, n_space)})
    lax.fori_loop(1, n_dp, greet, 0)

    @pl.when(level > 0)
    def _():
        pl.semaphore_signal(barrier, inc=1, device_id={SECTION: level - 1})

    @pl.when(level < n_section - 1)
    def _():
        pl.semaphore_signal(barrier, inc=1, device_id={SECTION: level + 1})

    def row_of(k, r):
        return stage[k, pl.ds(r, C, stride=ROWS), :]

    def lane(r, n=1):
        return slice(r * LANES, (r + n) * LANES)

    inner = lane(1, FULL)

    for ref in (x, xd, xs, xc):
        ref[:, :, lane(0)] = jnp.zeros((4, C, LANES), ref.dtype)
        ref[:, :, lane(FULL + 1)] = jnp.zeros((4, C, LANES), ref.dtype)
    c3e[:, :, lane(0)] = jnp.zeros((4, WIDE, LANES), c3e.dtype)
    c3e[:, :, lane(FULL + 1)] = jnp.zeros((4, WIDE, LANES), c3e.dtype)
    for ref in (skip_send, cot_send):
        ref[0] = jnp.zeros((C, PAIR), ref.dtype)
        ref[FULL + 1] = jnp.zeros((C, PAIR), ref.dtype)

    @pl.when(slab == 0)
    def _():
        x[0] = jnp.zeros((C, PADDED), x.dtype)
        xd[0] = jnp.zeros((C, PADDED), xd.dtype)

    @pl.when(slab == last)
    def _():
        x[3] = jnp.zeros((C, PADDED), x.dtype)
        xd[3] = jnp.zeros((C, PADDED), xd.dtype)

    loads[0].wait()
    stage[0] = loaded[0].astype(jnp.float32)
    for u in range(SPLIT):
        for v in range(FULL):
            x[1 + u, :, lane(1 + v)] = row_of(0, u * FULL + v).astype(jnp.bfloat16)
    loads[1].wait()
    stage[1] = loaded[1].astype(jnp.float32)
    for u in range(SPLIT):
        for v in range(FULL):
            cot_send[1 + v, :, lane(u)] = row_of(1, v * SPLIT + u).astype(jnp.bfloat16)
    loads[3].wait()
    stage[2] = loaded[2].astype(jnp.float32)
    for u in range(SPLIT):
        for v in range(FULL):
            xd[1 + u, :, lane(1 + v)] = row_of(2, v * SPLIT + u).astype(jnp.bfloat16)

    def halo(k, up):
        src_u, dst_u, peer = (2, 0, slab + 1) if up else (1, 3, slab - 1)
        ref = (x, xd)[k]
        n = 2 * k + (0 if up else 1)
        return pltpu.make_async_remote_copy(
            src_ref=ref.at[src_u, :, inner], dst_ref=ref.at[dst_u, :, inner],
            send_sem=halo_s.at[n], recv_sem=halo_r.at[n], device_id={SPACE: peer},
        )

    def halo_start(k):
        @pl.when(slab < last)
        def _():
            halo(k, True).start()

        @pl.when(slab > 0)
        def _():
            halo(k, False).start()

    def halo_arrived(k):
        @pl.when(slab > 0)
        def _():
            halo(k, True).wait_recv()

        @pl.when(slab < last)
        def _():
            halo(k, False).wait_recv()

    def regroup(sender, receiver, send_sem, recv_sem, own):
        def refs(source, target):
            at = pl.multiple_of((1 + source * SPLIT) * LANES, LANES)
            return (
                sender.at[pl.ds(target * SPLIT, SPLIT + 2)],
                receiver.at[:, :, pl.ds(at, PAIR)],
            )

        def copy(i):
            peer = lax.rem(slab + i, n_space)
            src, dst = refs(slab, peer)
            return pltpu.make_async_remote_copy(
                src_ref=src, dst_ref=dst, send_sem=send_sem.at[i - 1],
                recv_sem=recv_sem.at[i - 1], device_id={SPACE: peer},
            )

        def arrival(i):
            peer = lax.rem(slab - i + n_space, n_space)
            src, dst = refs(peer, slab)
            return pltpu.make_async_remote_copy(
                src_ref=src, dst_ref=dst, send_sem=send_sem.at[i - 1],
                recv_sem=recv_sem.at[i - 1], device_id={SPACE: peer},
            )

        return copy, arrival, pltpu.make_async_copy(*refs(slab, slab), own)

    cot_copy, cot_arrival, cot_own = regroup(cot_send, xc, cot_s, cot_r, own_sem.at[0])
    skip_copy, skip_arrival, skip_own = regroup(skip_send, xs, skip_s, skip_r, own_sem.at[1])

    pl.semaphore_wait(
        barrier, n_dp + n_space - 2 + lax.min(level, 1) + lax.min(n_section - 1 - level, 1)
    )
    halo_start(0)
    for i in range(1, n_space):
        cot_copy(i).start()
    cot_own.start()
    halo_start(1)

    for n in (6, 7, 8, 9):
        loads[n].wait()
    prm[...] = jnp.zeros((LANES, LANES), jnp.float32)
    for n in range(4):
        prm[n : n + 1, 0:C] = params[n]
    columns = prm[...].T
    e_gain, e_bias = columns[0:C, 0:1], columns[0:C, 1:2]
    d_gain, d_bias = columns[0:C, 2:3], columns[0:C, 3:4]
    pick = (
        lax.broadcasted_iota(jnp.int32, (C, 2 * C), 1)
        == lax.broadcasted_iota(jnp.int32, (C, 2 * C), 0) + C
    ).astype(jnp.bfloat16)
    loads[5].wait()
    for t in range(TAPS):
        tr_w[t] = dot_t(pick, dec_w[t]).astype(jnp.bfloat16)
    loads[4].wait()
    stage[3] = loaded[3].astype(jnp.float32)
    for u in range(SPLIT):
        for v in range(FULL):
            c3[u, :, lane(v)] = gather_taps(row_of(1, v * SPLIT + u))
            deep[v, :, lane(u)] = row_of(3, u * FULL + v)
    loads[2].wait()

    zero = jnp.zeros((C, LANES), jnp.float32)
    chunk = 2

    halo_arrived(0)
    first, second = zero, zero
    for u in range(SPLIT):
        for q in range(0, FULL, chunk):
            acc = jnp.zeros((WIDE, chunk * LANES), jnp.float32)
            for a in range(3):
                for b in range(3):
                    acc = acc + dot(enc_w[3 * a + b], x[u + a, :, lane(q + b, chunk)])
            for r in range(chunk):
                row = merge_taps(acc[:, lane(r)])
                pre[q + r, :, lane(u)] = row
                first = first + row
                second = second + row * row

    def stat_copy(n, i):
        k = n * (n_space - 1) + i - 1
        return pltpu.make_async_remote_copy(
            src_ref=stat_send.at[n], dst_ref=stat_got.at[n, slab],
            send_sem=stat_s.at[k], recv_sem=stat_r.at[k],
            device_id={SPACE: lax.rem(slab + i, n_space)},
        )

    def stat_arrival(n, i):
        k = n * (n_space - 1) + i - 1
        peer = lax.rem(slab - i + n_space, n_space)
        return pltpu.make_async_remote_copy(
            src_ref=stat_send.at[n], dst_ref=stat_got.at[n, peer],
            send_sem=stat_s.at[k], recv_sem=stat_r.at[k], device_id={SPACE: peer},
        )

    def send_stats(n, first, second):
        packed = pack_stats(first, second)
        stat_send[n] = packed
        for i in range(1, n_space):
            stat_copy(n, i).start()
        stat_got[n, slab] = packed
        return packed

    def all_stats(n):
        for i in range(1, n_space):
            stat_arrival(n, i).wait_recv()
        packed = stat_got[n, 0]
        for j in range(1, n_space):
            packed = packed + stat_got[n, j]
        one, two = unpack(packed, 16)
        return one * (1.0 / voxels), two * (1.0 / voxels)

    packed = send_stats(0, first, second)
    own_mean = unpack(packed, 16)[0] * (1.0 / cells)
    for v in range(FULL):
        for u in range(SPLIT):
            skip_send[1 + v, :, lane(u)] = (pre[v, :, lane(u)] - own_mean).astype(jnp.bfloat16)
    for i in range(1, n_space):
        skip_copy(i).start()
    skip_own.start()

    for i in range(1, n_space):
        cot_arrival(i).wait_recv()
    cot_own.wait()
    for u in range(4):
        for v in range(FULL):
            c3e[u, :, lane(1 + v)] = gather_taps(xc[u, :, lane(1 + v)].astype(jnp.float32))
    for u in range(SPLIT):
        for q in range(0, FULL, chunk):
            acc = jnp.zeros((C, chunk * LANES), jnp.float32)
            for a in range(3):
                for b in range(3):
                    acc = acc + dot(tr_w[3 * a + b], c3e[u + 2 - a, :, lane(q + 2 - b, chunk)])
            for r in range(chunk):
                sg[q + r, :, lane(u)] = acc[:, lane(r)].astype(jnp.bfloat16)

    e_mean, e_square = all_stats(0)
    e_scale = lax.rsqrt(e_square - e_mean * e_mean + EPS)

    def enc_hat_of(v, u):
        return (pre[v, :, lane(u)] - e_mean) * e_scale

    def gated_of(v, u, hat):
        upstream = sg[v, :, lane(u)].astype(jnp.float32) + deep[v, :, lane(u)]
        return jnp.where(e_gain * hat + e_bias > 0, upstream, 0.0) * e_gain

    first, second = zero, zero
    for v in range(FULL):
        for u in range(SPLIT):
            hat = enc_hat_of(v, u)
            gated = gated_of(v, u, hat)
            first = first + gated
            second = second + gated * hat
    send_stats(1, first, second)
    for v in range(FULL):
        for u in range(SPLIT):
            back[0, pl.ds(u * FULL + v, C, stride=ROWS), :] = jnp.maximum(
                e_gain * enc_hat_of(v, u) + e_bias, 0.0
            )
    enc_flat[...] = back[0].astype(jnp.bfloat16)

    lanes8 = lanes_of((8, LANES))
    per_peer = UNIT // n_dp

    def send_unit(n, left, right):
        for a in range(3):
            for b in range(3):
                acc = jnp.zeros((WIDE, C), jnp.float32)
                for u in range(SPLIT):
                    acc = acc + dot_t(left(u), right(u, a, b))
                t = 3 * a + b
                grads[n, t * WIDE : (t + 1) * WIDE, 0:C] = acc * grad_scale
        for p in range(n_dp):
            block = grads[n, pl.ds(p * per_peer, 8, stride=4), :]
            for g in range(1, 4):
                rows = grads[n, pl.ds(p * per_peer + g, 8, stride=4), :]
                block = jnp.where(lanes8 < 32 * g, block, pltpu.roll(rows, 32 * g, 1))
            terms[n, p] = block.astype(SEND)

        def start(i, carry):
            far_copy(n, i).start()
            return carry

        lax.fori_loop(1, n_dp, start, 0)

    def far_copy(n, i):
        peer = lax.rem(me + i * ORDER, n_dp)
        return pltpu.make_async_remote_copy(
            src_ref=terms.at[n, peer], dst_ref=arrived.at[n, me],
            send_sem=far_s.at[n, peer], recv_sem=far_r.at[n, me], device_id={DP: peer},
        )

    def far_arrival(n, i):
        peer = lax.rem(me - i * ORDER + n_dp * ORDER, n_dp)
        return peer, pltpu.make_async_remote_copy(
            src_ref=terms.at[n, peer], dst_ref=arrived.at[n, peer],
            send_sem=far_s.at[n, peer], recv_sem=far_r.at[n, peer], device_id={DP: peer},
        )

    halo_arrived(1)
    send_unit(1, lambda u: c3[u], lambda u, a, b: xd[u + b, :, lane(a, FULL)])

    gain = e_gain * e_scale
    for i in range(1, n_space):
        skip_arrival(i).wait_recv()
    skip_own.wait()
    for j in range(n_space):
        shift = gain * (unpack(stat_got[0, j], 16)[0] * (1.0 / cells) - e_mean) + e_bias
        for w in range(SPLIT):
            at = lane(1 + SPLIT * j + w)
            for u in range(4):
                act = jnp.maximum(gain * xs[u, :, at].astype(jnp.float32) + shift, 0.0)
                if u == 0:
                    act = jnp.where(slab > 0, act, 0.0)
                if u == 3:
                    act = jnp.where(slab < last, act, 0.0)
                xs[u, :, at] = act.astype(jnp.bfloat16)

    first, second = zero, zero
    for u in range(SPLIT):
        for q in range(0, FULL, chunk):
            acc = jnp.zeros((WIDE, chunk * LANES), jnp.float32)
            for a in range(3):
                for b in range(3):
                    at = lane(q + a, chunk)
                    joined = jnp.concatenate([xd[u + b, :, at], xs[u + b, :, at]], axis=0)
                    acc = acc + dot(dec_w[3 * a + b], joined)
            for r in range(chunk):
                row = merge_taps(acc[:, lane(r)])
                dec_pre[u, :, lane(q + r)] = row
                first = first + row
                second = second + row * row
    packed = send_stats(2, first, second)
    own_mean = unpack(packed, 16)[0] * (1.0 / cells)
    for u in range(SPLIT):
        for v in range(FULL):
            dec_raw[u, :, lane(v)] = (dec_pre[u, :, lane(v)] - own_mean).astype(jnp.bfloat16)

    def hand(k):
        src, dst, step = ((enc_flat, enc_out, 1), (dec_raw, dec_got, -1), (coef_send, coef_got, -1))[k]
        return pltpu.make_async_remote_copy(
            src_ref=src, dst_ref=dst, send_sem=hand_s.at[k], recv_sem=hand_r.at[k],
            device_id={SECTION: level + step},
        )

    @pl.when(level > 0)
    def _():
        hand(1).start()

    @pl.when(level < n_section - 1)
    def _():
        hand(0).start()

    g_mean, gh_mean = all_stats(1)
    for u in range(SPLIT):
        for v in range(FULL):
            hat = enc_hat_of(v, u)
            row = (gated_of(v, u, hat) - g_mean - hat * gh_mean) * e_scale
            row = row.astype(jnp.bfloat16).astype(jnp.float32)
            e3[u, :, lane(v)] = gather_taps(row)
    send_unit(0, lambda u: e3[u], lambda u, a, b: x[u + a, :, lane(b, FULL)])
    send_unit(2, lambda u: c3[u], lambda u, a, b: xs[u + b, :, lane(a, FULL)])

    d_mean, d_square = all_stats(2)
    d_gain = d_gain * lax.rsqrt(d_square - d_mean * d_mean + EPS)
    coef_send[...] = pack_pair(d_gain, d_gain * (own_mean - d_mean) + d_bias)

    @pl.when(level > 0)
    def _():
        hand(2).start()

    @pl.when(level == 0)
    def _():
        enc_out[...] = jnp.zeros(enc_out.shape, enc_out.dtype)

    for n in (1, 0, 2):
        def collect(i, acc):
            peer, copy = far_arrival(n, i)
            copy.wait_recv()
            return acc + arrived[n, peer].astype(jnp.float32)

        near_send[n] = lax.fori_loop(1, n_dp, collect, terms[n, me].astype(jnp.float32))

    def near_copy(i):
        return pltpu.make_async_remote_copy(
            src_ref=near_send, dst_ref=near_got.at[i - 1],
            send_sem=near_s.at[i - 1], recv_sem=near_r.at[i - 1],
            device_id={SPACE: lax.rem(slab + i, n_space)},
        )

    for i in range(1, n_space):
        near_copy(i).start()

    @pl.when(level < n_section - 1)
    def _():
        hand(1).wait_recv()
        hand(2).wait_recv()
        scale, shift = unpack(coef_got[...], 1)
        for u in range(SPLIT):
            for v in range(FULL):
                back[1, pl.ds(v * SPLIT + u, C, stride=ROWS), :] = jnp.maximum(
                    scale * dec_got[u, :, lane(v)].astype(jnp.float32) + shift, 0.0
                )
        dec_out[...] = back[1].astype(jnp.bfloat16)

    @pl.when(level == n_section - 1)
    def _():
        dec_out[...] = jnp.zeros(dec_out.shape, dec_out.dtype)

    acc = near_send[...]
    for i in range(1, n_space):
        near_copy(i).wait_recv()
        acc = acc + near_got[i - 1]
    total[...] = acc

    @pl.when(level > 0)
    def _():
        hand(0).wait_recv()
        hand(1).wait_send()
        hand(2).wait_send()

    @pl.when(level < n_section - 1)
    def _():
        hand(0).wait_send()

    @pl.when(slab < last)
    def _():
        for k in range(2):
            halo(k, True).wait_send()

    @pl.when(slab > 0)
    def _():
        for k in range(2):
            halo(k, False).wait_send()

    for i in range(1, n_space):
        for n in range(3):
            stat_copy(n, i).wait_send()
        cot_copy(i).wait_send()
        skip_copy(i).wait_send()
        near_copy(i).wait_send()
    for n in range(3):
        def drain(i, carry):
            far_copy(n, i).wait_send()
            return carry

        lax.fori_loop(1, n_dp, drain, 0)


def finish(n_space, enc_in, dec_in, sums, enc_hbm, dec_hbm, enc_grad, dec_grad, sems):
    slab = lax.axis_index(SPACE)
    copies = [
        pltpu.make_async_copy(enc_in, enc_hbm, sems.at[0]),
        pltpu.make_async_copy(dec_in, dec_hbm, sems.at[1]),
    ]
    for copy in copies:
        copy.start()

    def part(rows, out):
        flat = jnp.concatenate(rows, axis=1)
        width = out.shape[1]
        mine = flat[:, 0:width]
        for j in range(1, n_space):
            mine = jnp.where(slab == j, flat[:, j * width : (j + 1) * width], mine)
        out[...] = mine

    part([sums[0, r : r + 1, :] for r in range(7)], enc_grad)
    own, skip = sums[1], sums[2]
    group = lanes_of((8, LANES)) // C
    even = jnp.where(
        group == 0, own,
        jnp.where(
            group == 1, pltpu.roll(skip, 32, 1),
            jnp.where(group == 2, pltpu.roll(own, 32, 1), pltpu.roll(skip, 64, 1)),
        ),
    )
    odd = jnp.where(
        group == 0, pltpu.roll(own, 64, 1),
        jnp.where(
            group == 1, pltpu.roll(skip, 96, 1),
            jnp.where(group == 2, pltpu.roll(own, 96, 1), skip),
        ),
    )
    rows = []
    for r in range(7):
        rows += [even[r : r + 1, :], odd[r : r + 1, :]]
    part(rows, dec_grad)
    for copy in copies:
        copy.wait()


def body(
    enc_input, dec_input, dec_cotangent, deep_cotangent,
    enc_weight, dec_weight, enc_gain, enc_bias, dec_gain, dec_bias,
):
    n_section, n_dp, n_space = (lax.axis_size(a) for a in (SECTION, DP, SPACE))
    voxels = enc_input.shape[3] * n_space * enc_input.shape[4] * enc_input.shape[5]
    grad_scale = 1.0 / math.sqrt(n_dp * voxels)
    flat = (C * ROWS, LANES)
    vmem = pl.BlockSpec(memory_space=pltpu.VMEM)
    hbm = pl.BlockSpec(memory_space=pltpu.HBM)
    bf16, f32 = jnp.bfloat16, jnp.float32
    dma = pltpu.SemaphoreType.DMA
    others = n_space - 1
    enc_out, dec_out, total = pl.pallas_call(
        lambda *refs: kernel(n_section, n_dp, n_space, voxels, grad_scale, *refs),
        out_shape=(
            pltpu.VMEM(flat, bf16),
            pltpu.VMEM(flat, bf16),
            pltpu.VMEM((3, 8, LANES), f32),
        ),
        in_specs=[hbm] * 10,
        out_specs=(vmem, vmem, vmem),
        scratch_shapes=[
            pltpu.VMEM((4, *flat), bf16),
            pltpu.VMEM((TAPS, WIDE, C), bf16),
            pltpu.VMEM((TAPS, WIDE, 2 * C), bf16),
            pltpu.VMEM((4, 1, C), f32),
            pltpu.VMEM((4, *flat), f32),
            pltpu.VMEM((2, *flat), f32),
            pltpu.VMEM((4, C, PADDED), bf16),
            pltpu.VMEM((4, C, PADDED), bf16),
            pltpu.VMEM((4, C, PADDED), bf16),
            pltpu.VMEM((4, C, PADDED), bf16),
            pltpu.VMEM((FULL + 2, C, PAIR), bf16),
            pltpu.VMEM((SPLIT, WIDE, RUN), bf16),
            pltpu.VMEM((4, WIDE, PADDED), bf16),
            pltpu.VMEM((SPLIT, WIDE, RUN), bf16),
            pltpu.VMEM((FULL + 2, C, PAIR), bf16),
            pltpu.VMEM((FULL, C, PAIR), bf16),
            pltpu.VMEM((FULL, C, PAIR), f32),
            pltpu.VMEM((FULL, C, PAIR), f32),
            pltpu.VMEM((SPLIT, C, RUN), f32),
            pltpu.VMEM((LANES, LANES), f32),
            pltpu.VMEM((TAPS, C, WIDE), bf16),
            pltpu.VMEM((3, 8, LANES), f32),
            pltpu.VMEM((3, n_space, 8, LANES), f32),
            pltpu.VMEM((3, UNIT + 8, LANES), f32),
            pltpu.VMEM((3, n_dp, 8, LANES), SEND),
            pltpu.VMEM((3, n_dp, 8, LANES), SEND),
            pltpu.VMEM((3, 8, LANES), f32),
            pltpu.VMEM((others, 3, 8, LANES), f32),
            pltpu.VMEM(flat, bf16),
            pltpu.VMEM((SPLIT, C, RUN), bf16),
            pltpu.VMEM((SPLIT, C, RUN), bf16),
            pltpu.VMEM((8, LANES), f32),
            pltpu.VMEM((8, LANES), f32),
            dma((10,)),
            dma((4,)), dma((4,)),
            dma((3 * others,)), dma((3 * others,)),
            dma((others,)), dma((others,)),
            dma((others,)), dma((others,)),
            dma((2,)),
            dma((3,)), dma((3,)),
            dma((3, n_dp)), dma((3, n_dp)),
            dma((others,)), dma((others,)),
        ],
        compiler_params=pltpu.CompilerParams(
            collective_id=0, has_side_effects=True, vmem_limit_bytes=48 * 1024 * 1024
        ),
    )(
        *(
            pltpu.with_memory_space_constraint(array, pltpu.HBM)
            for array in (
                enc_input.reshape(flat), dec_input.reshape(flat), dec_cotangent.reshape(flat),
                deep_cotangent.reshape(flat), enc_weight.reshape(TAPS, WIDE, C),
                dec_weight.reshape(TAPS, WIDE, 2 * C), enc_gain, enc_bias, dec_gain, dec_bias,
            )
        )
    )
    enc_width, dec_width = UNIT * C // (n_dp * n_space), 2 * UNIT * C // (n_dp * n_space)
    enc_out, dec_out, enc_grad, dec_grad = pl.pallas_call(
        lambda *refs: finish(n_space, *refs),
        out_shape=(
            jax.ShapeDtypeStruct(flat, bf16),
            jax.ShapeDtypeStruct(flat, bf16),
            jax.ShapeDtypeStruct((1, enc_width), f32),
            jax.ShapeDtypeStruct((1, dec_width), f32),
        ),
        in_specs=[vmem] * 3,
        out_specs=(hbm, hbm, vmem, vmem),
        scratch_shapes=[dma((2,))],
        compiler_params=pltpu.CompilerParams(vmem_limit_bytes=4 * 1024 * 1024),
    )(enc_out, dec_out, total)
    return (
        enc_out.reshape(enc_input.shape), dec_out.reshape(dec_input.shape), enc_grad, dec_grad
    )


def solution(mesh):
    by_depth = P(SECTION, DP, None, SPACE, None, None)
    by_height = P(SECTION, DP, None, None, SPACE, None)
    whole3, whole1 = P(SECTION, None, None, None), P(SECTION, None)
    return jax.shard_map(
        body,
        mesh=mesh,
        in_specs=(by_depth, by_height, by_height, by_depth, whole3, whole3, *[whole1] * 4),
        out_specs=(by_depth, by_height, P(SECTION, (DP, SPACE)), P(SECTION, (DP, SPACE))),
        check_vma=False,
    )
```

time: 52.8 us -> 42.7 us (0.81)
  local copies, waits for them, and re-layouts: 8.9 us -> 0 us
  Pallas kernels: 42.9 us -> 41.9 us
    unnamed x22 -> x0, local copies, waits for them, and re-layouts: 7.47 us -> none
    pallas_call x1, Pallas kernels: 42.9 us -> 40.6 us  [body(): pl.pallas_call(lambda *refs: kernel(n_section, n_dp, n_space, voxels, gra...]
    pallas_call x0 -> x1, Pallas kernels: none -> 1.31 us  [body(): pl.pallas_call(lambda *refs: finish(n_space, *refs), out_shape=(jax.Shape...]
    dynamic_slice x2 -> x0, local copies, waits for them, and re-layouts: 1.16 us -> none  [the longest x1 0.59 us: body(): lax.dynamic_index_in_dim(dec_sums, slab, 0)]
where the time goes in v3:
time: 42.7 us; the launch traced here: 42.5 us
  Pallas kernels  41.9 us (98%)
  between operations  0.64 us (1%)
    pallas_call x1, Pallas kernels, body(): pl.pallas_call(lambda *refs: kernel(n_section, n_dp, n_space, voxels, gra...  40.6 us
    pallas_call x1, Pallas kernels, body(): pl.pallas_call(lambda *refs: finish(n_space, *refs), out_shape=(jax.Shape...  1.31 us

profile of v3, /device:TPU:1, one launch (start us, length us, event | category | flops | bytes accessed | tf_op | source)
XLA Modules:
  0.0 42.5 jit_solution(17256340008199338617)
XLA Ops:
  0.6 40.6 %shard_map.129 = (bf16[512,128]{1,0:T(8,128)(2,1)S(1)}, bf16[512,128]{1,0:T(8,128)(2,1)S(1)}, f32[3,8,128]{2,1,0:T(8,128)S(1)}) custom-call(bf16[512,128]{1,0:T(8,128)(2,1)} %bitcast.10, bf16[512,128]{1,0:T(8,128)(2,1)} %bitcast.11, bf16[512,128]{1,0:T(8,128)(2,1)} %bitcast.12, bf16[512,128]{1,0:T(8,128)(2,1)} %bitcast.13, bf16[9,96,32]{2,1,0:T(8,128)(2,1)} %bitcast.8, ...), custom_call_target="tpu_custom_call" | custom-call | tf_op jit(solution)/shard_map/pallas_call | solution.py:617
  41.2 1.3 %shard_map.130 = (bf16[512,128]{1,0:T(8,128)(2,1)}, bf16[512,128]{1,0:T(8,128)(2,1)}, f32[1,216]{1,0:T(1,128)}, f32[1,432]{1,0:T(1,128)}) custom-call(bf16[512,128]{1,0:T(8,128)(2,1)S(1)} %get-tuple-element.11.refs_0_, bf16[512,128]{1,0:T(8,128)(2,1)S(1)} %get-tuple-element.12.refs_1_, f32[3,8,128]{2,1,0:T(8,128)S(1)} %get-tuple-element.13.refs_2_), custom_call_target="tpu_custom_call" | custom-call | tf_op jit(solution)/shard_map/pallas_call | solution.py:684

commit v4 on v3

--- a/solution.py
+++ b/solution.py
@@ -24,6 +24,7 @@
 TAPS = 9
 WIDE = 3 * C
 UNIT = TAPS * WIDE
+RING = 8
 ORDER = 11
 SEND = jnp.bfloat16
 
@@ -102,7 +103,7 @@
     prm, tr_w, stat_send, stat_got, grads, terms, arrived, near_send, near_got,
     enc_flat, dec_raw, dec_got, coef_send, coef_got,
     load_s, halo_s, halo_r, stat_s, stat_r, skip_s, skip_r, cot_s, cot_r, own_sem,
-    hand_s, hand_r, far_s, far_r, near_s, near_r,
+    hand_s, hand_r, far_s, far_r, near_s, near_r, known,
 ):
     me = lax.axis_index(DP)
     slab = lax.axis_index(SPACE)
@@ -125,13 +126,25 @@
 
     barrier = pltpu.get_barrier_semaphore()
 
-    def greet(i, carry):
-        pl.semaphore_signal(barrier, inc=1, device_id={DP: lax.rem(me + i, n_dp)})
-        return carry
+    ring = min(RING, n_dp)
+    far, near = lax.div(me, ring), lax.rem(me, ring)
+
+    def along(step):
+        return far * ring + lax.rem(near + step + ring, ring)
+
+    def across(step):
+        return lax.rem(far + step + n_dp // ring, n_dp // ring) * ring + near
+
+    def tell(sem, peers):
+        for peer in peers:
+            pl.semaphore_signal(sem, inc=1, device_id={DP: peer})
+
+    def heard(n):
+        pl.semaphore_wait(known.at[n], 2)
 
     for i in range(1, n_space):
         pl.semaphore_signal(barrier, inc=1, device_id={SPACE: lax.rem(slab + i, n_space)})
-    lax.fori_loop(1, n_dp, greet, 0)
+    tell(barrier, (along(1), along(-1), across(1), across(-1)))
 
     @pl.when(level > 0)
     def _():
@@ -241,13 +254,14 @@
     skip_copy, skip_arrival, skip_own = regroup(skip_send, xs, skip_s, skip_r, own_sem.at[1])
 
     pl.semaphore_wait(
-        barrier, n_dp + n_space - 2 + lax.min(level, 1) + lax.min(n_section - 1 - level, 1)
+        barrier, 4 + n_space - 1 + lax.min(level, 1) + lax.min(n_section - 1 - level, 1)
     )
     halo_start(0)
     for i in range(1, n_space):
         cot_copy(i).start()
     cot_own.start()
     halo_start(1)
+    tell(known.at[0], (along(1), along(-1)))
 
     for n in (6, 7, 8, 9):
         loads[n].wait()
@@ -271,6 +285,8 @@
             c3[u, :, lane(v)] = gather_taps(row_of(1, v * SPLIT + u))
             deep[v, :, lane(u)] = row_of(3, u * FULL + v)
     loads[2].wait()
+    heard(0)
+    tell(known.at[1], (along(2), along(-2)))
 
     zero = jnp.zeros((C, LANES), jnp.float32)
     chunk = 2
@@ -330,6 +346,8 @@
     for i in range(1, n_space):
         skip_copy(i).start()
     skip_own.start()
+    heard(1)
+    tell(known.at[2], (across(1), across(-1)))
 
     for i in range(1, n_space):
         cot_arrival(i).wait_recv()
@@ -345,6 +363,9 @@
                     acc = acc + dot(tr_w[3 * a + b], c3e[u + 2 - a, :, lane(q + 2 - b, chunk)])
             for r in range(chunk):
                 sg[q + r, :, lane(u)] = acc[:, lane(r)].astype(jnp.bfloat16)
+
+    heard(2)
+    tell(known.at[3], (across(1), across(-1)))
 
     e_mean, e_square = all_stats(0)
     e_scale = lax.rsqrt(e_square - e_mean * e_mean + EPS)
@@ -399,16 +420,16 @@
         peer = lax.rem(me + i * ORDER, n_dp)
         return pltpu.make_async_remote_copy(
             src_ref=terms.at[n, peer], dst_ref=arrived.at[n, me],
-            send_sem=far_s.at[n, peer], recv_sem=far_r.at[n, me], device_id={DP: peer},
-        )
-
-    def far_arrival(n, i):
-        peer = lax.rem(me - i * ORDER + n_dp * ORDER, n_dp)
-        return peer, pltpu.make_async_remote_copy(
-            src_ref=terms.at[n, peer], dst_ref=arrived.at[n, peer],
-            send_sem=far_s.at[n, peer], recv_sem=far_r.at[n, peer], device_id={DP: peer},
-        )
-
+            send_sem=far_s.at[n], recv_sem=far_r.at[n], device_id={DP: peer},
+        )
+
+    def far_all(n):
+        return pltpu.make_async_remote_copy(
+            src_ref=terms.at[n, pl.ds(0, n_dp - 1)], dst_ref=arrived.at[n, pl.ds(0, n_dp - 1)],
+            send_sem=far_s.at[n], recv_sem=far_r.at[n], device_id={DP: along(1)},
+        )
+
+    heard(3)
     halo_arrived(1)
     send_unit(1, lambda u: c3[u], lambda u, a, b: xd[u + b, :, lane(a, FULL)])
 
@@ -486,12 +507,12 @@
         enc_out[...] = jnp.zeros(enc_out.shape, enc_out.dtype)
 
     for n in (1, 0, 2):
-        def collect(i, acc):
-            peer, copy = far_arrival(n, i)
-            copy.wait_recv()
-            return acc + arrived[n, peer].astype(jnp.float32)
-
-        near_send[n] = lax.fori_loop(1, n_dp, collect, terms[n, me].astype(jnp.float32))
+        far_all(n).wait_recv()
+        arrived[n, me] = terms[n, me]
+        sums = [arrived[n, p].astype(jnp.float32) for p in range(n_dp)]
+        while len(sums) > 1:
+            sums = [a + b for a, b in zip(sums[::2], sums[1::2])]
+        near_send[n] = sums[0]
 
     def near_copy(i):
         return pltpu.make_async_remote_copy(
@@ -552,11 +573,7 @@
         skip_copy(i).wait_send()
         near_copy(i).wait_send()
     for n in range(3):
-        def drain(i, carry):
-            far_copy(n, i).wait_send()
-            return carry
-
-        lax.fori_loop(1, n_dp, drain, 0)
+        far_all(n).wait_send()
 
 
 def finish(n_space, enc_in, dec_in, sums, enc_hbm, dec_hbm, enc_grad, dec_grad, sems):
@@ -664,8 +681,9 @@
             dma((others,)), dma((others,)),
             dma((2,)),
             dma((3,)), dma((3,)),
-            dma((3, n_dp)), dma((3, n_dp)),
+            dma((3,)), dma((3,)),
             dma((others,)), dma((others,)),
+            pltpu.SemaphoreType.REGULAR((4,)),
         ],
         compiler_params=pltpu.CompilerParams(
             collective_id=0, has_side_effects=True, vmem_limit_bytes=48 * 1024 * 1024

time: 42.7 us -> 38.4 us (0.90)
  Pallas kernels: 41.9 us -> 37.6 us
    pallas_call x1, Pallas kernels: 40.6 us -> 36.3 us  [body(): pl.pallas_call(lambda *refs: kernel(n_section, n_dp, n_space, voxels, gra...]
where the time goes in v4:
time: 38.4 us; the launch traced here: 38.3 us
  Pallas kernels  37.6 us (98%)
  between operations  0.64 us (2%)
    pallas_call x1, Pallas kernels, body(): pl.pallas_call(lambda *refs: kernel(n_section, n_dp, n_space, voxels, gra...  36.3 us
    pallas_call x1, Pallas kernels, body(): pl.pallas_call(lambda *refs: finish(n_space, *refs), out_shape=(jax.Shape...  1.31 us

profile of v4, /device:TPU:1, one launch (start us, length us, event | category | flops | bytes accessed | tf_op | source)
XLA Modules:
  0.0 38.3 jit_solution(3660453114178987926)
XLA Ops:
  0.6 36.3 %shard_map.129 = (bf16[512,128]{1,0:T(8,128)(2,1)S(1)}, bf16[512,128]{1,0:T(8,128)(2,1)S(1)}, f32[3,8,128]{2,1,0:T(8,128)S(1)}) custom-call(bf16[512,128]{1,0:T(8,128)(2,1)} %bitcast.10, bf16[512,128]{1,0:T(8,128)(2,1)} %bitcast.11, bf16[512,128]{1,0:T(8,128)(2,1)} %bitcast.12, bf16[512,128]{1,0:T(8,128)(2,1)} %bitcast.13, bf16[9,96,32]{2,1,0:T(8,128)(2,1)} %bitcast.8, ...), custom_call_target="tpu_custom_call" | custom-call | tf_op jit(solution)/shard_map/pallas_call | solution.py:634
  36.9 1.3 %shard_map.130 = (bf16[512,128]{1,0:T(8,128)(2,1)}, bf16[512,128]{1,0:T(8,128)(2,1)}, f32[1,216]{1,0:T(1,128)}, f32[1,432]{1,0:T(1,128)}) custom-call(bf16[512,128]{1,0:T(8,128)(2,1)S(1)} %get-tuple-element.11.refs_0_, bf16[512,128]{1,0:T(8,128)(2,1)S(1)} %get-tuple-element.12.refs_1_, f32[3,8,128]{2,1,0:T(8,128)S(1)} %get-tuple-element.13.refs_2_), custom_call_target="tpu_custom_call" | custom-call | tf_op jit(solution)/shard_map/pallas_call | solution.py:702

commit v5 on v4

--- a/solution.py
+++ b/solution.py
@@ -25,7 +25,6 @@
 WIDE = 3 * C
 UNIT = TAPS * WIDE
 RING = 8
-ORDER = 11
 SEND = jnp.bfloat16
 
 
@@ -100,7 +99,7 @@
     enc_out, dec_out, total,
     loaded, enc_w, dec_w, params,
     stage, back, x, xd, xs, xc, cot_send, c3, c3e, e3, skip_send, sg, deep, pre, dec_pre,
-    prm, tr_w, stat_send, stat_got, grads, terms, arrived, near_send, near_got,
+    prm, tr_w, wide_e, wide_d, stat_send, stat_got, grads, terms, arrived, near_send, near_got,
     enc_flat, dec_raw, dec_got, coef_send, coef_got,
     load_s, halo_s, halo_r, stat_s, stat_r, skip_s, skip_r, cot_s, cot_r, own_sem,
     hand_s, hand_r, far_s, far_r, near_s, near_r, known,
@@ -175,11 +174,15 @@
     def _():
         x[0] = jnp.zeros((C, PADDED), x.dtype)
         xd[0] = jnp.zeros((C, PADDED), xd.dtype)
+        xc[0] = jnp.zeros((C, PADDED), xc.dtype)
+        xs[0] = jnp.zeros((C, PADDED), xs.dtype)
 
     @pl.when(slab == last)
     def _():
         x[3] = jnp.zeros((C, PADDED), x.dtype)
         xd[3] = jnp.zeros((C, PADDED), xd.dtype)
+        xc[3] = jnp.zeros((C, PADDED), xc.dtype)
+        xs[3] = jnp.zeros((C, PADDED), xs.dtype)
 
     loads[0].wait()
     stage[0] = loaded[0].astype(jnp.float32)
@@ -225,40 +228,53 @@
             halo(k, False).wait_recv()
 
     def regroup(sender, receiver, send_sem, recv_sem, own):
-        def refs(source, target):
+        def refs(source, target, first, count):
             at = pl.multiple_of((1 + source * SPLIT) * LANES, LANES)
             return (
-                sender.at[pl.ds(target * SPLIT, SPLIT + 2)],
-                receiver.at[:, :, pl.ds(at, PAIR)],
+                sender.at[pl.ds(target * SPLIT + first, count)],
+                receiver.at[pl.ds(first, count), :, pl.ds(at, PAIR)],
             )
 
-        def copy(i):
-            peer = lax.rem(slab + i, n_space)
-            src, dst = refs(slab, peer)
+        def remote(i, peer, source, target, first, count):
+            src, dst = refs(source, target, first, count)
             return pltpu.make_async_remote_copy(
                 src_ref=src, dst_ref=dst, send_sem=send_sem.at[i - 1],
                 recv_sem=recv_sem.at[i - 1], device_id={SPACE: peer},
             )
 
-        def arrival(i):
-            peer = lax.rem(slab - i + n_space, n_space)
-            src, dst = refs(peer, slab)
-            return pltpu.make_async_remote_copy(
-                src_ref=src, dst_ref=dst, send_sem=send_sem.at[i - 1],
-                recv_sem=recv_sem.at[i - 1], device_id={SPACE: peer},
-            )
-
-        return copy, arrival, pltpu.make_async_copy(*refs(slab, slab), own)
-
-    cot_copy, cot_arrival, cot_own = regroup(cot_send, xc, cot_s, cot_r, own_sem.at[0])
-    skip_copy, skip_arrival, skip_own = regroup(skip_send, xs, skip_s, skip_r, own_sem.at[1])
+        def copies(act):
+            for i in range(1, n_space):
+                peer = lax.rem(slab + i, n_space)
+                by_end(peer, lambda *cut: act(remote(i, peer, slab, peer, *cut)))
+
+        def arrivals():
+            for i in range(1, n_space):
+                peer = lax.rem(slab - i + n_space, n_space)
+                by_end(slab, lambda *cut: remote(i, peer, peer, slab, *cut).wait_recv())
+
+        return copies, arrivals, pltpu.make_async_copy(*refs(slab, slab, 0, SPLIT + 2), own)
+
+    def by_end(target, act):
+        @pl.when(target == 0)
+        def _():
+            act(1, SPLIT + 1)
+
+        @pl.when(target == last)
+        def _():
+            act(0, SPLIT + 1)
+
+        @pl.when((target > 0) & (target < last))
+        def _():
+            act(0, SPLIT + 2)
+
+    cot_copies, cot_arrivals, cot_own = regroup(cot_send, xc, cot_s, cot_r, own_sem.at[0])
+    skip_copies, skip_arrivals, skip_own = regroup(skip_send, xs, skip_s, skip_r, own_sem.at[1])
 
     pl.semaphore_wait(
         barrier, 4 + n_space - 1 + lax.min(level, 1) + lax.min(n_section - 1 - level, 1)
     )
     halo_start(0)
-    for i in range(1, n_space):
-        cot_copy(i).start()
+    cot_copies(lambda copy: copy.start())
     cot_own.start()
     halo_start(1)
     tell(known.at[0], (along(1), along(-1)))
@@ -278,13 +294,16 @@
     loads[5].wait()
     for t in range(TAPS):
         tr_w[t] = dot_t(pick, dec_w[t]).astype(jnp.bfloat16)
+    loads[2].wait()
+    for k in range(3):
+        wide_e[k] = jnp.concatenate([enc_w[3 * k + b] for b in range(3)], axis=1)
+        wide_d[k] = jnp.concatenate([dec_w[3 * a + k] for a in range(3)], axis=1)
     loads[4].wait()
     stage[3] = loaded[3].astype(jnp.float32)
     for u in range(SPLIT):
         for v in range(FULL):
             c3[u, :, lane(v)] = gather_taps(row_of(1, v * SPLIT + u))
             deep[v, :, lane(u)] = row_of(3, u * FULL + v)
-    loads[2].wait()
     heard(0)
     tell(known.at[1], (along(2), along(-2)))
 
@@ -297,8 +316,8 @@
         for q in range(0, FULL, chunk):
             acc = jnp.zeros((WIDE, chunk * LANES), jnp.float32)
             for a in range(3):
-                for b in range(3):
-                    acc = acc + dot(enc_w[3 * a + b], x[u + a, :, lane(q + b, chunk)])
+                three = [x[u + a, :, lane(q + b, chunk)] for b in range(3)]
+                acc = acc + dot(wide_e[a], jnp.concatenate(three, axis=0))
             for r in range(chunk):
                 row = merge_taps(acc[:, lane(r)])
                 pre[q + r, :, lane(u)] = row
@@ -343,14 +362,12 @@
     for v in range(FULL):
         for u in range(SPLIT):
             skip_send[1 + v, :, lane(u)] = (pre[v, :, lane(u)] - own_mean).astype(jnp.bfloat16)
-    for i in range(1, n_space):
-        skip_copy(i).start()
+    skip_copies(lambda copy: copy.start())
     skip_own.start()
     heard(1)
     tell(known.at[2], (across(1), across(-1)))
 
-    for i in range(1, n_space):
-        cot_arrival(i).wait_recv()
+    cot_arrivals()
     cot_own.wait()
     for u in range(4):
         for v in range(FULL):
@@ -410,14 +427,21 @@
                 block = jnp.where(lanes8 < 32 * g, block, pltpu.roll(rows, 32 * g, 1))
             terms[n, p] = block.astype(SEND)
 
-        def start(i, carry):
-            far_copy(n, i).start()
-            return carry
-
-        lax.fori_loop(1, n_dp, start, 0)
-
-    def far_copy(n, i):
-        peer = lax.rem(me + i * ORDER, n_dp)
+        for dx, dz in hops:
+            far_copy(n, dx, dz).start()
+
+    columns_of = n_dp // ring
+
+    def steps(d, n):
+        return min(d, n - d)
+
+    hops = sorted(
+        ((dx, dz) for dx in range(columns_of) for dz in range(ring) if dx or dz),
+        key=lambda hop: (-steps(hop[0], columns_of) - steps(hop[1], ring), hop[0] * 3 % 4, hop[1] * 5 % 8),
+    )
+
+    def far_copy(n, dx, dz):
+        peer = lax.rem(far + dx, columns_of) * ring + lax.rem(near + dz, ring)
         return pltpu.make_async_remote_copy(
             src_ref=terms.at[n, peer], dst_ref=arrived.at[n, me],
             send_sem=far_s.at[n], recv_sem=far_r.at[n], device_id={DP: peer},
@@ -434,8 +458,7 @@
     send_unit(1, lambda u: c3[u], lambda u, a, b: xd[u + b, :, lane(a, FULL)])
 
     gain = e_gain * e_scale
-    for i in range(1, n_space):
-        skip_arrival(i).wait_recv()
+    skip_arrivals()
     skip_own.wait()
     for j in range(n_space):
         shift = gain * (unpack(stat_got[0, j], 16)[0] * (1.0 / cells) - e_mean) + e_bias
@@ -453,11 +476,12 @@
     for u in range(SPLIT):
         for q in range(0, FULL, chunk):
             acc = jnp.zeros((WIDE, chunk * LANES), jnp.float32)
-            for a in range(3):
-                for b in range(3):
+            for b in range(3):
+                three = []
+                for a in range(3):
                     at = lane(q + a, chunk)
-                    joined = jnp.concatenate([xd[u + b, :, at], xs[u + b, :, at]], axis=0)
-                    acc = acc + dot(dec_w[3 * a + b], joined)
+                    three += [xd[u + b, :, at], xs[u + b, :, at]]
+                acc = acc + dot(wide_d[b], jnp.concatenate(three, axis=0))
             for r in range(chunk):
                 row = merge_taps(acc[:, lane(r)])
                 dec_pre[u, :, lane(q + r)] = row
@@ -569,9 +593,9 @@
     for i in range(1, n_space):
         for n in range(3):
             stat_copy(n, i).wait_send()
-        cot_copy(i).wait_send()
-        skip_copy(i).wait_send()
         near_copy(i).wait_send()
+    cot_copies(lambda copy: copy.wait_send())
+    skip_copies(lambda copy: copy.wait_send())
     for n in range(3):
         far_all(n).wait_send()
 
@@ -662,6 +686,8 @@
             pltpu.VMEM((SPLIT, C, RUN), f32),
             pltpu.VMEM((LANES, LANES), f32),
             pltpu.VMEM((TAPS, C, WIDE), bf16),
+            pltpu.VMEM((3, WIDE, 3 * C), bf16),
+            pltpu.VMEM((3, WIDE, 6 * C), bf16),
             pltpu.VMEM((3, 8, LANES), f32),
             pltpu.VMEM((3, n_space, 8, LANES), f32),
             pltpu.VMEM((3, UNIT + 8, LANES), f32),

time: 38.4 us -> 36.9 us (0.961)
  Pallas kernels: 37.6 us -> 36.1 us
    pallas_call x1, Pallas kernels: 36.3 us -> 34.8 us  [body(): pl.pallas_call(lambda *refs: kernel(n_section, n_dp, n_space, voxels, gra...]
where the time goes in v5:
time: 36.9 us; the launch traced here: 36.8 us
  Pallas kernels  36.1 us (98%)
  between operations  0.64 us (2%)
    pallas_call x1, Pallas kernels, body(): pl.pallas_call(lambda *refs: kernel(n_section, n_dp, n_space, voxels, gra...  34.8 us
    pallas_call x1, Pallas kernels, body(): pl.pallas_call(lambda *refs: finish(n_space, *refs), out_shape=(jax.Shape...  1.31 us

profile of v5, /device:TPU:1, one launch (start us, length us, event | category | flops | bytes accessed | tf_op | source)
XLA Modules:
  0.0 36.8 jit_solution(2621795240848184187)
XLA Ops:
  0.6 34.8 %shard_map.129 = (bf16[512,128]{1,0:T(8,128)(2,1)S(1)}, bf16[512,128]{1,0:T(8,128)(2,1)S(1)}, f32[3,8,128]{2,1,0:T(8,128)S(1)}) custom-call(bf16[512,128]{1,0:T(8,128)(2,1)} %bitcast.10, bf16[512,128]{1,0:T(8,128)(2,1)} %bitcast.11, bf16[512,128]{1,0:T(8,128)(2,1)} %bitcast.12, bf16[512,128]{1,0:T(8,128)(2,1)} %bitcast.13, bf16[9,96,32]{2,1,0:T(8,128)(2,1)} %bitcast.8, ...), custom_call_target="tpu_custom_call" | custom-call | tf_op jit(solution)/shard_map/pallas_call | solution.py:658
  35.5 1.3 %shard_map.130 = (bf16[512,128]{1,0:T(8,128)(2,1)}, bf16[512,128]{1,0:T(8,128)(2,1)}, f32[1,216]{1,0:T(1,128)}, f32[1,432]{1,0:T(1,128)}) custom-call(bf16[512,128]{1,0:T(8,128)(2,1)S(1)} %get-tuple-element.11.refs_0_, bf16[512,128]{1,0:T(8,128)(2,1)S(1)} %get-tuple-element.12.refs_1_, f32[3,8,128]{2,1,0:T(8,128)S(1)} %get-tuple-element.13.refs_2_), custom_call_target="tpu_custom_call" | custom-call | tf_op jit(solution)/shard_map/pallas_call | solution.py:728

commit v6 on v5

--- a/solution.py
+++ b/solution.py
@@ -472,6 +472,20 @@
                     act = jnp.where(slab < last, act, 0.0)
                 xs[u, :, at] = act.astype(jnp.bfloat16)
 
+    send_unit(2, lambda u: c3[u], lambda u, a, b: xs[u + b, :, lane(a, FULL)])
+
+    def hand(k):
+        src, dst, step = (
+            (enc_flat, enc_out, 1),
+            (dec_raw.at[0], dec_got.at[0], -1),
+            (dec_raw.at[1], dec_got.at[1], -1),
+            (coef_send, coef_got, -1),
+        )[k]
+        return pltpu.make_async_remote_copy(
+            src_ref=src, dst_ref=dst, send_sem=hand_s.at[k], recv_sem=hand_r.at[k],
+            device_id={SECTION: level + step},
+        )
+
     first, second = zero, zero
     for u in range(SPLIT):
         for q in range(0, FULL, chunk):
@@ -487,22 +501,17 @@
                 dec_pre[u, :, lane(q + r)] = row
                 first = first + row
                 second = second + row * row
-    packed = send_stats(2, first, second)
-    own_mean = unpack(packed, 16)[0] * (1.0 / cells)
-    for u in range(SPLIT):
+        if u == 0:
+            centre = jnp.sum(first, axis=1, keepdims=True) * (SPLIT / cells)
+        else:
+            send_stats(2, first, second)
         for v in range(FULL):
-            dec_raw[u, :, lane(v)] = (dec_pre[u, :, lane(v)] - own_mean).astype(jnp.bfloat16)
-
-    def hand(k):
-        src, dst, step = ((enc_flat, enc_out, 1), (dec_raw, dec_got, -1), (coef_send, coef_got, -1))[k]
-        return pltpu.make_async_remote_copy(
-            src_ref=src, dst_ref=dst, send_sem=hand_s.at[k], recv_sem=hand_r.at[k],
-            device_id={SECTION: level + step},
-        )
-
-    @pl.when(level > 0)
-    def _():
-        hand(1).start()
+            dec_raw[u, :, lane(v)] = (dec_pre[u, :, lane(v)] - centre).astype(jnp.bfloat16)
+
+        @pl.when(level > 0)
+        def _():
+            hand(1 + u).start()
+
 
     @pl.when(level < n_section - 1)
     def _():
@@ -516,42 +525,43 @@
             row = row.astype(jnp.bfloat16).astype(jnp.float32)
             e3[u, :, lane(v)] = gather_taps(row)
     send_unit(0, lambda u: e3[u], lambda u, a, b: x[u + a, :, lane(b, FULL)])
-    send_unit(2, lambda u: c3[u], lambda u, a, b: xs[u + b, :, lane(a, FULL)])
-
     d_mean, d_square = all_stats(2)
     d_gain = d_gain * lax.rsqrt(d_square - d_mean * d_mean + EPS)
-    coef_send[...] = pack_pair(d_gain, d_gain * (own_mean - d_mean) + d_bias)
+    coef_send[...] = pack_pair(d_gain, d_gain * (centre - d_mean) + d_bias)
 
     @pl.when(level > 0)
     def _():
-        hand(2).start()
+        hand(3).start()
 
     @pl.when(level == 0)
     def _():
         enc_out[...] = jnp.zeros(enc_out.shape, enc_out.dtype)
 
-    for n in (1, 0, 2):
+    def near_copy(n, i):
+        units = pl.ds(1, 2) if n else pl.ds(0, 1)
+        k = i - 1 + (n_space - 1) * min(n, 1)
+        return pltpu.make_async_remote_copy(
+            src_ref=near_send.at[units], dst_ref=near_got.at[i - 1, units],
+            send_sem=near_s.at[k], recv_sem=near_r.at[k],
+            device_id={SPACE: lax.rem(slab + i, n_space)},
+        )
+
+    for n in (1, 2, 0):
         far_all(n).wait_recv()
         arrived[n, me] = terms[n, me]
         sums = [arrived[n, p].astype(jnp.float32) for p in range(n_dp)]
         while len(sums) > 1:
             sums = [a + b for a, b in zip(sums[::2], sums[1::2])]
         near_send[n] = sums[0]
-
-    def near_copy(i):
-        return pltpu.make_async_remote_copy(
-            src_ref=near_send, dst_ref=near_got.at[i - 1],
-            send_sem=near_s.at[i - 1], recv_sem=near_r.at[i - 1],
-            device_id={SPACE: lax.rem(slab + i, n_space)},
-        )
-
-    for i in range(1, n_space):
-        near_copy(i).start()
+        if n != 1:
+            for i in range(1, n_space):
+                near_copy(n, i).start()
 
     @pl.when(level < n_section - 1)
     def _():
         hand(1).wait_recv()
         hand(2).wait_recv()
+        hand(3).wait_recv()
         scale, shift = unpack(coef_got[...], 1)
         for u in range(SPLIT):
             for v in range(FULL):
@@ -566,7 +576,8 @@
 
     acc = near_send[...]
     for i in range(1, n_space):
-        near_copy(i).wait_recv()
+        for n in (2, 0):
+            near_copy(n, i).wait_recv()
         acc = acc + near_got[i - 1]
     total[...] = acc
 
@@ -575,6 +586,7 @@
         hand(0).wait_recv()
         hand(1).wait_send()
         hand(2).wait_send()
+        hand(3).wait_send()
 
     @pl.when(level < n_section - 1)
     def _():
@@ -593,7 +605,8 @@
     for i in range(1, n_space):
         for n in range(3):
             stat_copy(n, i).wait_send()
-        near_copy(i).wait_send()
+        for n in (2, 0):
+            near_copy(n, i).wait_send()
     cot_copies(lambda copy: copy.wait_send())
     skip_copies(lambda copy: copy.wait_send())
     for n in range(3):
@@ -706,9 +719,9 @@
             dma((others,)), dma((others,)),
             dma((others,)), dma((others,)),
             dma((2,)),
+            dma((4,)), dma((4,)),
             dma((3,)), dma((3,)),
-            dma((3,)), dma((3,)),
-            dma((others,)), dma((others,)),
+            dma((2 * others,)), dma((2 * others,)),
             pltpu.SemaphoreType.REGULAR((4,)),
         ],
         compiler_params=pltpu.CompilerParams(

time: 36.9 us -> 36.8 us (level)
  no operation moved by 1% of the time
where the time goes in v6:
time: 36.8 us; the launch traced here: 36.6 us
  Pallas kernels  36 us (98%)
  between operations  0.64 us (2%)
    pallas_call x1, Pallas kernels, body(): pl.pallas_call(lambda *refs: kernel(n_section, n_dp, n_space, voxels, gra...  34.7 us
    pallas_call x1, Pallas kernels, body(): pl.pallas_call(lambda *refs: finish(n_space, *refs), out_shape=(jax.Shape...  1.31 us

profile of v6, /device:TPU:1, one launch (start us, length us, event | category | flops | bytes accessed | tf_op | source)
XLA Modules:
  0.0 36.6 jit_solution(5759725919990570573)
XLA Ops:
  0.6 34.7 %shard_map.129 = (bf16[512,128]{1,0:T(8,128)(2,1)S(1)}, bf16[512,128]{1,0:T(8,128)(2,1)S(1)}, f32[3,8,128]{2,1,0:T(8,128)S(1)}) custom-call(bf16[512,128]{1,0:T(8,128)(2,1)} %bitcast.10, bf16[512,128]{1,0:T(8,128)(2,1)} %bitcast.11, bf16[512,128]{1,0:T(8,128)(2,1)} %bitcast.12, bf16[512,128]{1,0:T(8,128)(2,1)} %bitcast.13, bf16[9,96,32]{2,1,0:T(8,128)(2,1)} %bitcast.8, ...), custom_call_target="tpu_custom_call" | custom-call | tf_op jit(solution)/shard_map/pallas_call | solution.py:671
  35.3 1.3 %shard_map.130 = (bf16[512,128]{1,0:T(8,128)(2,1)}, bf16[512,128]{1,0:T(8,128)(2,1)}, f32[1,216]{1,0:T(1,128)}, f32[1,432]{1,0:T(1,128)}) custom-call(bf16[512,128]{1,0:T(8,128)(2,1)S(1)} %get-tuple-element.11.refs_0_, bf16[512,128]{1,0:T(8,128)(2,1)S(1)} %get-tuple-element.12.refs_1_, f32[3,8,128]{2,1,0:T(8,128)S(1)} %get-tuple-element.13.refs_2_), custom_call_target="tpu_custom_call" | custom-call | tf_op jit(solution)/shard_map/pallas_call | solution.py:741

commit v7 on v6

--- a/solution.py
+++ b/solution.py
@@ -189,17 +189,6 @@
     for u in range(SPLIT):
         for v in range(FULL):
             x[1 + u, :, lane(1 + v)] = row_of(0, u * FULL + v).astype(jnp.bfloat16)
-    loads[1].wait()
-    stage[1] = loaded[1].astype(jnp.float32)
-    for u in range(SPLIT):
-        for v in range(FULL):
-            cot_send[1 + v, :, lane(u)] = row_of(1, v * SPLIT + u).astype(jnp.bfloat16)
-    loads[3].wait()
-    stage[2] = loaded[2].astype(jnp.float32)
-    for u in range(SPLIT):
-        for v in range(FULL):
-            xd[1 + u, :, lane(1 + v)] = row_of(2, v * SPLIT + u).astype(jnp.bfloat16)
-
     def halo(k, up):
         src_u, dst_u, peer = (2, 0, slab + 1) if up else (1, 3, slab - 1)
         ref = (x, xd)[k]
@@ -274,10 +263,21 @@
         barrier, 4 + n_space - 1 + lax.min(level, 1) + lax.min(n_section - 1 - level, 1)
     )
     halo_start(0)
+    tell(known.at[0], (along(1), along(-1)))
+    loads[1].wait()
+    stage[1] = loaded[1].astype(jnp.float32)
+    for u in range(SPLIT):
+        for v in range(FULL):
+            cot_send[1 + v, :, lane(u)] = row_of(1, v * SPLIT + u).astype(jnp.bfloat16)
     cot_copies(lambda copy: copy.start())
     cot_own.start()
+    loads[3].wait()
+    stage[2] = loaded[2].astype(jnp.float32)
+    for u in range(SPLIT):
+        for v in range(FULL):
+            xd[1 + u, :, lane(1 + v)] = row_of(2, v * SPLIT + u).astype(jnp.bfloat16)
+
     halo_start(1)
-    tell(known.at[0], (along(1), along(-1)))
 
     for n in (6, 7, 8, 9):
         loads[n].wait()
@@ -308,7 +308,7 @@
     tell(known.at[1], (along(2), along(-2)))
 
     zero = jnp.zeros((C, LANES), jnp.float32)
-    chunk = 2
+    chunk = 4
 
     halo_arrived(0)
     first, second = zero, zero
@@ -437,7 +437,7 @@
 
     hops = sorted(
         ((dx, dz) for dx in range(columns_of) for dz in range(ring) if dx or dz),
-        key=lambda hop: (-steps(hop[0], columns_of) - steps(hop[1], ring), hop[0] * 3 % 4, hop[1] * 5 % 8),
+        key=lambda hop: (-steps(hop[1], ring), -steps(hop[0], columns_of), hop[1]),
     )
 
     def far_copy(n, dx, dz):

time: 36.8 us -> 36.8 us (level)
  no operation moved by 1% of the time
where the time goes in v7:
time: 36.8 us; the launch traced here: 36.6 us
  Pallas kernels  36 us (98%)
  between operations  0.64 us (2%)
    pallas_call x1, Pallas kernels, body(): pl.pallas_call(lambda *refs: kernel(n_section, n_dp, n_space, voxels, gra...  34.7 us
    pallas_call x1, Pallas kernels, body(): pl.pallas_call(lambda *refs: finish(n_space, *refs), out_shape=(jax.Shape...  1.31 us

profile of v7, /device:TPU:1, one launch (start us, length us, event | category | flops | bytes accessed | tf_op | source)
XLA Modules:
  0.0 36.6 jit_solution(17412968280383540268)
XLA Ops:
  0.6 34.7 %shard_map.129 = (bf16[512,128]{1,0:T(8,128)(2,1)S(1)}, bf16[512,128]{1,0:T(8,128)(2,1)S(1)}, f32[3,8,128]{2,1,0:T(8,128)S(1)}) custom-call(bf16[512,128]{1,0:T(8,128)(2,1)} %bitcast.10, bf16[512,128]{1,0:T(8,128)(2,1)} %bitcast.11, bf16[512,128]{1,0:T(8,128)(2,1)} %bitcast.12, bf16[512,128]{1,0:T(8,128)(2,1)} %bitcast.13, bf16[9,96,32]{2,1,0:T(8,128)(2,1)} %bitcast.8, ...), custom_call_target="tpu_custom_call" | custom-call | tf_op jit(solution)/shard_map/pallas_call | solution.py:671
  35.3 1.3 %shard_map.130 = (bf16[512,128]{1,0:T(8,128)(2,1)}, bf16[512,128]{1,0:T(8,128)(2,1)}, f32[1,216]{1,0:T(1,128)}, f32[1,432]{1,0:T(1,128)}) custom-call(bf16[512,128]{1,0:T(8,128)(2,1)S(1)} %get-tuple-element.11.refs_0_, bf16[512,128]{1,0:T(8,128)(2,1)S(1)} %get-tuple-element.12.refs_1_, f32[3,8,128]{2,1,0:T(8,128)S(1)} %get-tuple-element.13.refs_2_), custom_call_target="tpu_custom_call" | custom-call | tf_op jit(solution)/shard_map/pallas_call | solution.py:741
